TPU v7x, 64 devices: a 2x2x8 block of a 4x4x8 slice. The times are simulated.
64 devices in a mesh: dp: 4 (over x, y), sp: 16 (over z, core).
Axes of the slice: x: 2, y: 2, z: 8, core: 2. Of those that a mesh axis runs over, the one named last changes fastest.
The devices are a block of a 4x4x8 slice.
Arguments:
- pair_rep: float32 [1024, 256, 128], P(('dp', 'sp')), parts along dimension 0
- w_qkvg_s: bfloat16 [128, 512], replicated
- w_bias_s: bfloat16 [4, 128], replicated
- w_out_s: bfloat16 [128, 128], replicated
- w_qkvg_e: bfloat16 [128, 512], replicated
- w_bias_e: bfloat16 [4, 128], replicated
- w_out_e: bfloat16 [128, 128], replicated
- w_one: bfloat16 [128, 512], replicated
- w_two: bfloat16 [512, 128], replicated
Outputs:
- output: float32 [1024, 256, 128], P(('dp', 'sp')), parts along dimension 0
There are 4 independent parts. A program takes and returns all parts, laid end to end along the dimension named above; an argument that names none is the same for every part.
All inputs are finite; a program needn't handle non-finite values.
Results may differ from a plain program's by a relative error of at most 0.0105142.
Values are sent between devices in bfloat16 or wider.
A program may use at most 768 MiB of HBM per device.

v0:
```python
import jax
import jax.numpy as jnp
from jax import lax
from jax.sharding import PartitionSpec as P

LN_EPS = 1e-5
SCORE_CAP = 2 ** 23


def layer_norm(values):
    vals_f = values.astype(jnp.float32)
    mean_c = jnp.mean(vals_f, axis=-1, keepdims=True)
    centered = vals_f - mean_c
    variance = jnp.mean(centered * centered, axis=-1, keepdims=True)
    return (centered * lax.rsqrt(variance + LN_EPS)).astype(jnp.bfloat16)


def project(normed, w_qkvg, num_heads):
    channels = w_qkvg.shape[0]
    projected = jnp.dot(normed, w_qkvg, preferred_element_type=jnp.float32)
    split_shape = normed.shape[:-1] + (num_heads, channels // num_heads)
    queries = projected[..., :channels].astype(jnp.bfloat16).reshape(split_shape)
    key_vecs = projected[..., channels:2 * channels].astype(jnp.bfloat16).reshape(split_shape)
    val_vecs = projected[..., 2 * channels:3 * channels].astype(jnp.bfloat16).reshape(split_shape)
    gate_vals = jax.nn.sigmoid(projected[..., 3 * channels:]).reshape(split_shape)
    return queries, key_vecs, val_vecs, gate_vals


def attend(queries, key_vecs, val_vecs, gate_vals, bias_full, w_out, score_form, mix_form):
    head_dim = queries.shape[-1]
    scores = jnp.einsum(score_form, queries, key_vecs, preferred_element_type=jnp.float32)
    scores = scores * head_dim ** -0.5 + bias_full.astype(jnp.float32)
    attn_prob = jax.nn.softmax(scores, axis=-1).astype(jnp.bfloat16)
    attn_out = jnp.einsum(mix_form, attn_prob, val_vecs, preferred_element_type=jnp.float32)
    gated_out = (attn_out * gate_vals).astype(jnp.bfloat16)
    merged = gated_out.reshape(gated_out.shape[:-2] + (w_out.shape[0],))
    return jnp.dot(merged, w_out, preferred_element_type=jnp.float32)


def transition(resid_in, w_one, w_two):
    hidden = jax.nn.relu(jnp.dot(layer_norm(resid_in), w_one, preferred_element_type=jnp.float32))
    return jnp.dot(hidden.astype(jnp.bfloat16), w_two, preferred_element_type=jnp.float32)


def block_size(total_len, per_item):
    return max(candidate for candidate in range(1, total_len + 1) if total_len % candidate == 0 and (candidate == 1 or candidate * per_item <= SCORE_CAP))


def solution(mesh):
    row_spec = P(('dp', 'sp'), None, None)

    def local_fn(pair_loc, w_qkvg_s, w_bias_s, w_out_s, w_qkvg_e, w_bias_e, w_out_e, w_one, w_two):
        num_rows, seq_len, channels = pair_loc.shape
        num_heads = w_bias_s.shape[0]
        blk_rows = block_size(num_rows, num_heads * seq_len * seq_len)
        normed = layer_norm(pair_loc)
        bias_loc = jnp.einsum('hc,jkc->hjk', w_bias_s, normed, preferred_element_type=jnp.float32).astype(jnp.bfloat16)
        bias_s = lax.all_gather(bias_loc, 'sp', axis=1, tiled=True)

        def start_block(block_idx):
            normed_blk = lax.dynamic_slice_in_dim(normed, block_idx * blk_rows, blk_rows, axis=0)
            queries, key_vecs, val_vecs, gate_vals = project(normed_blk, w_qkvg_s, num_heads)
            return attend(queries, key_vecs, val_vecs, gate_vals, bias_s, w_out_s, 'rjhd,rkhd->rhjk', 'rhjk,rkhd->rjhd')

        start_upd = lax.map(start_block, jnp.arange(num_rows // blk_rows))
        pair_one = pair_loc + start_upd.reshape(num_rows, seq_len, channels)
        col_major = lax.all_to_all(pair_one.astype(jnp.bfloat16), 'sp', 1, 0, tiled=True)
        normed_c = layer_norm(col_major)
        bias_loc_e = jnp.einsum('hc,kic->hik', w_bias_e, normed_c, preferred_element_type=jnp.float32).astype(jnp.bfloat16)
        bias_e = lax.all_gather(bias_loc_e, 'sp', axis=1, tiled=True)

        def end_block(block_idx):
            normed_blk = lax.dynamic_slice_in_dim(normed_c, block_idx * blk_rows, blk_rows, axis=1)
            pair_blk = lax.dynamic_slice_in_dim(col_major, block_idx * blk_rows, blk_rows, axis=1)
            queries, key_vecs, val_vecs, gate_vals = project(normed_blk, w_qkvg_e, num_heads)
            end_upd = attend(queries, key_vecs, val_vecs, gate_vals, bias_e, w_out_e, 'ijhd,kjhd->jhik', 'jhik,kjhd->ijhd')
            pair_two = pair_blk.astype(jnp.float32) + end_upd
            return (end_upd + transition(pair_two, w_one, w_two)).astype(jnp.bfloat16)

        delta_blocks = lax.map(end_block, jnp.arange(num_rows // blk_rows))
        delta_cols = jnp.moveaxis(delta_blocks, 0, 1).reshape(seq_len, num_rows, channels)
        delta_rows = lax.all_to_all(delta_cols, 'sp', 0, 1, tiled=True)
        return pair_one + delta_rows.astype(jnp.float32)

    return jax.shard_map(local_fn, mesh=mesh, in_specs=(row_spec, P(), P(), P(), P(), P(), P(), P(), P()), out_specs=row_spec, check_vma=False)
```

profile of v0, /device:TPU:21, one launch (start us, length us, event | category | flops | bytes accessed | tf_op | source)
XLA Modules:
  0.0 207.6 jit_solution(9269355806230457243)
XLA Ops:
  0.0 2.4 %reduce_sum.76 = f32[16,256]{1,0:T(8,128)S(1)} reduce(f32[16,256,128]{2,1,0:T(8,128)} %param.9, f32[]{:T(128)} %constant.38.clone.1), dimensions={2}, to_apply=%region_0.0 | reduce | flops 520192 | bytes 2113540 | tf_op jit(solution)/shard_map/reduce_sum | solution.py:12
  2.4 1.3 multiply_reduce_fusion.2
  3.7 1.5 fusion.27
  5.2 24.1 %all_gather.6 = bf16[4,256,256]{2,0,1:T(4,128)(2,1)S(1)} all-gather(bf16[4,16,256]{2,0,1:T(4,128)(2,1)S(1)} %fusion.27), channel_id=1, replica_groups=mesh['dp'=4,'sp'=16] {'sp'}, dimensions={1}, use_global_device_ids=true | all-gather | bytes 557056 | tf_op jit(solution)/shard_map/all_gather | solution.py:58
  29.3 0.1 copy_convert_fusion.1
  29.4 1.4 copy.163
  30.8 4.0 %fusion.52 = (bf16[16,256,512]{2,1,0:T(8,128)(2,1)S(1)}, f32[16,256,512]{2,1,0:T(8,128)}) fusion(bf16[128,512]{1,0:T(8,128)(2,1)S(1)} %copy-done, f32[16,256,128]{2,1,0:T(8,128)S(1)} %copy-done.2, f32[16,256]{1,0:T(8,128)S(1)} %add_rsqrt_fusion.2, f32[16,256]{1,0:T(8,128)S(1)} %broadcast_multiply_fusion.2), kind=kOutput, calls=%fused_computation.78 | convolution fusion | flops 540540928 | bytes 14843904 | tf_op jit(solution)/shard_map/while/body/eval_jaxpr/dot_general | solution.py:20
  34.8 2.2 %fusion.51 = (bf16[16,256,128]{2,1,0:T(8,128)(2,1)}, bf16[16,256,128]{2,1,0:T(8,128)(2,1)}, bf16[16,256,128]{2,1,0:T(8,128)(2,1)S(1)}) fusion(bf16[16,256,512]{2,1,0:T(8,128)(2,1)S(1)} %get-tuple-element.49), kind=kLoop, calls=%fused_computation.77 | loop fusion | bytes 6291456 | tf_op jit(solution)/shard_map/while/body/eval_jaxpr/slice | solution.py:23
  37.0 2.3 %copy.161 = bf16[16,256,128]{1,2,0:T(8,128)(2,1)} copy(bf16[16,256,128]{2,1,0:T(8,128)(2,1)} %get-tuple-element.44) | data formatting | bytes 2097152 | tf_op jit(solution)/shard_map/while/body/eval_jaxpr/slice | solution.py:23
  39.3 2.3 %copy.160 = bf16[16,256,128]{1,2,0:T(8,128)(2,1)} copy(bf16[16,256,128]{2,1,0:T(8,128)(2,1)} %get-tuple-element.45) | data formatting | bytes 2097152 | tf_op jit(solution)/shard_map/while/body/eval_jaxpr/slice | solution.py:22
  41.6 1.3 copy.159
  42.9 3.5 %fusion.23 = f32[16,256,128]{2,1,0:T(8,128)} fusion(f32[16,256,512]{2,1,0:T(8,128)} %get-tuple-element.50), kind=kLoop, calls=%fused_computation.29 | loop fusion | flops 1572864 | bytes 4194304 | tf_op jit(solution)/shard_map/while/body/eval_jaxpr/div | solution.py:25
  46.4 3.0 %copy.165 = f32[16,256,128]{1,2,0:T(8,128)} copy(f32[16,256,128]{2,1,0:T(8,128)} %fusion.23) | data formatting | bytes 4194304 | tf_op jit(solution)/shard_map/while/body/eval_jaxpr/div | solution.py:25
  49.4 10.0 %fusion.53 = (f32[16,4,256]{2,1,0:T(4,128)S(1)}, f32[16,4,256,256]{2,3,1,0:T(8,128)}) fusion(bf16[16,256,4,32]{1,3,2,0:T(8,128)(2,1)} %bitcast.96, bf16[16,256,4,32]{1,3,2,0:T(8,128)(2,1)} %bitcast.94, f32[4,256,256]{1,2,0:T(8,128)S(1)} %copy-done.8), kind=kOutput, calls=%fused_computation.79 | convolution fusion | flops 285212928 | bytes 19988480 | tf_op jit(solution)/shard_map/while/body/eval_jaxpr/sub | solution.py:33
  59.5 8.2 %fusion.25 = bf16[16,256,4,32]{1,3,2,0:T(8,128)(2,1)S(1)} fusion(f32[16,256,4,32]{1,3,2,0:T(8,128)} %bitcast.91, bf16[16,256,4,32]{1,3,2,0:T(8,128)(2,1)} %bitcast.97, f32[16,4,256,256]{2,3,1,0:T(8,128)} %get-tuple-element.62, f32[16,4,256]{2,1,0:T(4,128)S(1)} %get-tuple-element.60), kind=kOutput, calls=%fused_computation.36 | convolution fusion | flops 277872640 | bytes 21037056 | tf_op jit(solution)/shard_map/while/body/eval_jaxpr/rhjk,rkhd->rjhd/dot_general | solution.py:34
  67.7 1.8 fusion.54
  69.5 0.7 copy.167
  70.2 30.6 %all_to_all.8 = bf16[16,256,128]{2,0,1:T(8,128)(2,1)S(1)} all-to-all(bf16[16,256,128]{2,0,1:T(8,128)(2,1)S(1)} %copy.167), channel_id=1, replica_groups=mesh['dp'=4,'sp'=16] {'sp'}, dimensions={1} | all-to-all | bytes 2097152 | tf_op jit(solution)/shard_map/all_to_all | solution.py:67
  100.8 0.3 convert_bitcast_fusion.1
  101.1 0.6 fusion.28
  101.8 1.3 multiply_reduce_fusion.1
  103.1 0.2 copy.169
  103.4 1.7 multiply_convert_fusion.1
  105.1 2.5 %fusion.26 = bf16[4,16,256]{1,0,2:T(4,128)(2,1)S(1)} fusion(bf16[256,16,128]{2,1,0:T(8,128)(2,1)S(1)} %multiply_convert_fusion.1, bf16[4,128]{1,0:T(4,128)(2,1)S(1)} %copy-done.13), kind=kOutput, calls=%fused_computation.46 | convolution fusion | flops 4210688 | bytes 1082368 | tf_op jit(solution)/shard_map/hc,kic->hik/dot_general | solution.py:69
  107.6 0.2 copy.178
  107.8 16.6 %all_gather.7 = bf16[4,256,256]{2,0,1:T(4,128)(2,1)S(1)} all-gather(bf16[4,16,256]{2,0,1:T(4,128)(2,1)S(1)} %copy.178), channel_id=1, replica_groups=mesh['dp'=4,'sp'=16] {'sp'}, dimensions={1}, use_global_device_ids=true | all-gather | bytes 557056 | tf_op jit(solution)/shard_map/all_gather | solution.py:70
  124.4 1.1 copy_convert_fusion
  125.5 2.6 %copy.180 = f32[4,256,256]{1,2,0:T(8,128)} copy(f32[4,256,256]{2,1,0:T(8,128)} %copy_convert_fusion) | data formatting | bytes 2097152 | tf_op jit(solution)/shard_map/while/body/eval_jaxpr/convert_element_type | solution.py:32
  128.1 1.9 copy.185
  130.0 4.5 %fusion.55 = (bf16[256,16,512]{2,0,1:T(8,128)(2,1)S(1)}, f32[256,16,512]{2,0,1:T(8,128)}) fusion(bf16[128,512]{1,0:T(8,128)(2,1)S(1)} %copy-done.9, bf16[256,16,128]{2,1,0:T(8,128)(2,1)S(1)} %multiply_convert_fusion.1), kind=kOutput, calls=%fused_computation.81 | convolution fusion | flops 538968064 | bytes 13762560 | tf_op jit(solution)/shard_map/while/body/eval_jaxpr/dot_general | solution.py:20
  134.4 0.9 fusion.50
  135.3 1.3 copy.177
  136.7 1.3 copy.176
  138.0 1.3 copy.175
  139.3 2.1 %fusion.20 = f32[256,16,128]{2,0,1:T(8,128)S(1)} fusion(f32[256,16,512]{2,0,1:T(8,128)} %get-tuple-element.67), kind=kLoop, calls=%fused_computation.25 | loop fusion | flops 1572864 | bytes 4194304 | tf_op jit(solution)/shard_map/while/body/eval_jaxpr/div | solution.py:25
  141.5 1.8 copy.182
  143.3 10.2 %fusion.56 = (f32[16,4,256]{2,1,0:T(4,128)S(1)}, f32[16,4,256,256]{2,3,1,0:T(8,128)}) fusion(bf16[256,16,4,32]{0,3,2,1:T(8,128)(2,1)} %bitcast.98, bf16[256,16,4,32]{0,3,2,1:T(8,128)(2,1)} %bitcast.95, f32[4,256,256]{1,2,0:T(8,128)S(1)} %copy-done.7), kind=kOutput, calls=%fused_computation.82 | convolution fusion | flops 285212928 | bytes 19988480 | tf_op jit(solution)/shard_map/while/body/eval_jaxpr/sub | solution.py:33
  153.5 7.8 %fusion.24 = bf16[256,16,4,32]{0,3,2,1:T(8,128)(2,1)S(1)} fusion(f32[256,16,4,32]{0,3,2,1:T(8,128)S(1)} %bitcast.92, bf16[256,16,4,32]{0,3,2,1:T(8,128)(2,1)} %bitcast.99, f32[16,4,256,256]{2,3,1,0:T(8,128)} %get-tuple-element.69, f32[16,4,256]{2,1,0:T(4,128)S(1)} %get-tuple-element.68), kind=kOutput, calls=%fused_computation.33 | convolution fusion | flops 277872640 | bytes 21037056 | tf_op jit(solution)/shard_map/while/body/eval_jaxpr/jhik,kjhd->ijhd/dot_general | solution.py:34
  161.3 1.9 fusion.49
  163.3 1.3 copy-done.5
  164.6 0.2 multiply_reduce_fusion
  164.9 4.8 %add_convert_fusion = bf16[256,16,128]{0,2,1:T(8,128)(2,1)S(1)} fusion(f32[256,16,128]{0,2,1:T(8,128)} %get-tuple-element.70, f32[256,16,128]{0,2,1:T(8,128)} %copy-done.5, f32[256,16]{0,1:T(8,128)S(1)} %add_rsqrt_fusion.1, f32[256,16]{0,1:T(8,128)S(1)} %broadcast_multiply_fusion.1, bf16[512,128]{1,0:T(8,128)(2,1)S(1)} %copy-done.14, ...), kind=kOutput, calls=%fused_computation.37 | convolution fusion | flops 1080557568 | bytes 5537792 | tf_op jit(solution)/shard_map/while/body/eval_jaxpr/dot_general | solution.py:42
  169.6 1.1 copy.188
  170.7 33.4 %all_to_all.9 = bf16[256,16,128]{2,1,0:T(8,128)(2,1)S(1)} all-to-all(bf16[256,16,128]{2,1,0:T(8,128)(2,1)S(1)} %copy.188), channel_id=1, replica_groups=mesh['dp'=4,'sp'=16] {'sp'}, dimensions={0} | all-to-all | bytes 2097152 | tf_op jit(solution)/shard_map/all_to_all | solution.py:82
  204.1 0.2 convert_bitcast_fusion
  204.4 0.2 copy.189
  204.6 1.4 copy-done.3
  206.0 1.6 bitcast_add_fusion
  (38 shorter events, 0.2 us)
Async XLA Ops:
  0.0 30.8 %copy-start = (bf16[128,512]{1,0:T(8,128)(2,1)S(1)}, bf16[128,512]{1,0:T(8,128)(2,1)}, u32[]{:S(2)}) copy-start(bf16[128,512]{1,0:T(8,128)(2,1)} %param.10) | copy-start | bytes 393220
  0.0 2.4 %copy-start.2 = (f32[16,256,128]{2,1,0:T(8,128)S(1)}, f32[16,256,128]{2,1,0:T(8,128)}, u32[]{:S(2)}) copy-start(f32[16,256,128]{2,1,0:T(8,128)} %param.9) | copy-start | bytes 6291460
  0.0 3.7 %copy-start.12 = (bf16[4,128]{1,0:T(4,128)(2,1)S(1)}, bf16[4,128]{1,0:T(4,128)(2,1)}, u32[]{:S(2)}) copy-start(bf16[4,128]{1,0:T(4,128)(2,1)} %param.11) | copy-start | bytes 3076
  46.4 3.0 %copy-start.8 = (f32[4,256,256]{1,2,0:T(8,128)S(1)}, f32[4,256,256]{1,2,0:T(8,128)}, u32[]{:S(2)}) copy-start(f32[4,256,256]{1,2,0:T(8,128)} %copy.163) | copy-start | bytes 3145732
  59.4 8.2 %copy-start.10 = (bf16[128,128]{1,0:T(8,128)(2,1)S(1)}, bf16[128,128]{1,0:T(8,128)(2,1)}, u32[]{:S(2)}) copy-start(bf16[128,128]{1,0:T(8,128)(2,1)} %param.12) | copy-start | bytes 98308
  103.3 1.8 copy-start.13
  128.1 1.9 copy-start.9
  141.5 1.8 copy-start.7
  143.3 10.2 %copy-start.6 = (f32[256,16,128]{0,2,1:T(8,128)S(1)}, f32[256,16,128]{0,2,1:T(8,128)}, u32[]{:S(2)}) copy-start(f32[256,16,128]{0,2,1:T(8,128)} %copy.182) | copy-start | bytes 6291460
  153.5 7.8 %copy-start.4 = (f32[256,16,128]{0,2,1:T(8,128)S(1)}, f32[256,16,128]{0,2,1:T(8,128)}, u32[]{:S(2)}) copy-start(f32[256,16,128]{0,2,1:T(8,128)} %copy.185) | copy-start | bytes 6291460
  153.5 7.8 %copy-start.11 = (bf16[128,128]{1,0:T(8,128)(2,1)S(1)}, bf16[128,128]{1,0:T(8,128)(2,1)}, u32[]{:S(2)}) copy-start(bf16[128,128]{1,0:T(8,128)(2,1)} %param.15) | copy-start | bytes 98308
  163.3 1.3 copy-start.5
  163.3 1.6 copy-start.14
  163.3 1.6 copy-start.15
  204.4 1.6 copy-start.3
  204.6 3.0 %copy-start.1 = (bf16[128,512]{1,0:T(8,128)(2,1)S(1)}, bf16[128,512]{1,0:T(8,128)(2,1)}, u32[]{:S(2)}) copy-start(bf16[128,512]{1,0:T(8,128)(2,1)} %param.10) | copy-start | bytes 393220
where the time goes:
time: 208 us
  blocking collectives  105 us (50%)
  matrix products  57.2 us (28%)
  local copies, waits for them, and re-layouts  28.9 us (14%)
  other arithmetic  16.5 us (8%)
    all_to_all x1, blocking collectives, local_fn(): delta_rows = lax.all_to_all(delta_cols, 'sp', 0, 1, tiled=True)  33.4 us
    all_to_all x1, blocking collectives, local_fn(): lax.all_to_all(pair_one.astype(jnp.bfloat16), 'sp', 1, 0, tiled=True)  30.6 us
    all_gather x1, blocking collectives, local_fn(): bias_s = lax.all_gather(bias_loc, 'sp', axis=1, tiled=True)  24.1 us
    sub x2, matrix products, attend(): attn_prob = jax.nn.softmax(scores, axis=-1).astype(jnp.bfloat16)  20.2 us
    all_gather x1, blocking collectives, local_fn(): bias_e = lax.all_gather(bias_loc_e, 'sp', axis=1, tiled=True)  16.6 us
    dot_general x2, matrix products, attend(): jnp.einsum(mix_form, attn_prob, val_vecs, preferred_element_type=jnp.floa...  16 us
    dot_general x2, matrix products, project(): projected = jnp.dot(normed, w_qkvg, preferred_element_type=jnp.float32)  8.44 us
    slice x4, local copies, waits for them, and re-layouts, project(): projected[..., channels:2 * channels].astype(jnp.bfloat16)  6.76 us

commit v1 on v0

v1 whole, which is shorter than its diff:
```python
import functools

import jax
import jax.numpy as jnp
from jax import lax
from jax.experimental import pallas as pl
from jax.experimental.pallas import tpu as pltpu
from jax.sharding import PartitionSpec as P

LN_EPS = 1e-5
F32, BF16 = jnp.float32, jnp.bfloat16
MESH = pl.DeviceIdType.MESH
AXIS = "sp"
CORES = 2
ROW_UNROLL = 2
COL_GROUP = 4
COL_UNROLL = 2


def norm(vals):
    mean_c = jnp.mean(vals, axis=-1, keepdims=True)
    centered = vals - mean_c
    variance = jnp.mean(centered * centered, axis=-1, keepdims=True)
    return (centered * lax.rsqrt(variance + LN_EPS)).astype(BF16)


def mm(a, b, ca=1, cb=0):
    return lax.dot_general(a, b, (((ca,), (cb,)), ((), ())), preferred_element_type=F32)


def sigmoid(x):
    return 1.0 / (1.0 + jnp.exp(-x))


def kernel(n, rows, seq, heads, z_ref, wp_s, wb_s, wo_s, wp_e, wb_e, wo_e, w1, w2,
           z1_ref, drecv,
           u_s, q_s, kt_s, v_s, g_s, bacc, brecv, bias_f, hsend, ht, erecv, bias_e, dsend, wt_e,
           b_ss, b_rs, bf_ss, e_ss, e_rs, ef_ss, h_ss, h_rs, d_ss, d_rs):
    chan = wo_s.shape[0]
    hd = chan // heads
    scale = hd ** -0.5
    chips = n // CORES
    me = lax.axis_index(AXIS)
    chip, core = me // CORES, lax.rem(me, CORES)
    partner = chip * CORES + (CORES - 1 - core)
    hrows = heads * rows

    def remote(src, dst, ss, rs, dev):
        return pltpu.make_async_remote_copy(src_ref=src, dst_ref=dst, send_sem=ss, recv_sem=rs,
                                            device_id={AXIS: dev}, device_id_type=MESH)

    barrier = pltpu.get_barrier_semaphore()
    for off in range(1, n):
        pl.semaphore_signal(barrier, 1, device_id={AXIS: lax.rem(me + off, n)}, device_id_type=MESH)

    def spread(wb):
        wide = wb[...].astype(F32)
        return jnp.concatenate([jnp.broadcast_to(wide[h:h + 1], (rows, chan)) for h in range(heads)], axis=0)

    row_of = lax.rem(lax.broadcasted_iota(jnp.int32, (hrows, chan), 0), rows)
    lane_head = lax.broadcasted_iota(jnp.int32, (1, chan), 1) // hd

    def pair_bias(get_row, put_row, wb, out):
        wide = spread(wb)
        bacc[...] = jnp.zeros_like(bacc)

        def step(i, carry):
            total = None
            for t in range(2):
                r = 2 * i + t
                u = norm(get_row(r))
                if put_row is not None:
                    put_row(r, u)
                picked = jnp.where(row_of == r, wide, 0.0).astype(BF16)
                part = mm(picked, u, 1, 1)
                total = part if total is None else total + part
            bacc[...] += total
            return carry

        lax.fori_loop(0, rows // 2, step, 0)
        out[me] = bacc[...].astype(BF16)

    def bias_copy(buf, ss, rs, dev):
        return remote(buf.at[me], buf.at[me], ss.at[dev], rs.at[me], dev)

    def bias_send(buf, ss, rs):
        bias_copy(buf, ss, rs, partner).start()
        for dist in range(1, chips):
            off = (dist + 1) // 2 if dist % 2 else chips - dist // 2
            bias_copy(buf, ss, rs, lax.rem(chip + off, chips) * CORES + core).start()

    def bias_wait(buf, ss, rs, src):
        remote(buf.at[src], buf.at[src], ss.at[src], rs.at[src], partner).wait_recv()

    def forward(buf, ss, rs, c):
        src = c * CORES + core
        return remote(buf.at[src], buf.at[src], ss.at[c], rs.at[src], partner)

    def bias_drain(buf, ss, rs, fss):
        bias_copy(buf, ss, rs, partner).wait_send()
        for dist in range(1, chips):
            c = lax.rem(chip + dist, chips)
            bias_copy(buf, ss, rs, c * CORES + core).wait_send()
            forward(buf, fss, rs, c).wait_send()

    def put_u(r, u):
        u_s[r] = u

    pair_bias(lambda r: z_ref[r], put_u, wb_s, brecv)
    pl.semaphore_wait(barrier, n - 1)
    bias_send(brecv, b_ss, b_rs)

    wk_t = wp_s[:, chan:2 * chan].astype(F32).T.astype(BF16)

    def project(i, carry):
        for t in range(2):
            r = 2 * i + t
            u = u_s[r]
            pr = mm(u, wp_s[...])
            q_s[r] = pr[:, :chan].astype(BF16)
            kt_s[r] = mm(wk_t, u, 1, 1).astype(BF16)
            v_s[r] = pr[:, 2 * chan:3 * chan].astype(BF16)
            g_s[r] = sigmoid(pr[:, 3 * chan:])
        return carry

    lax.fori_loop(0, rows // 2, project, 0)

    blk = CORES * rows
    nq = 2 * blk

    def chips_of(p):
        return lax.rem(chip + chips - p, chips), lax.rem(chip + p + 1, chips)

    def fetch_bias(p):
        for c in chips_of(p):
            @pl.when(c != chip)
            def _():
                bias_wait(brecv, b_ss, b_rs, c * CORES + core)
                forward(brecv, bf_ss, b_rs, c).start()

    fetch_bias(0)

    def start_pair(p, carry):
        ca, cb = chips_of(p)
        for c in (ca, cb):
            bias_wait(brecv, b_ss, b_rs, c * CORES + (CORES - 1 - core))
        devs = [c * CORES + s for c in (ca, cb) for s in range(CORES)]
        for h in range(heads):
            for k, dev in enumerate(devs):
                bias_f[h * nq + k * rows:h * nq + (k + 1) * rows, :] = brecv[dev, h * rows:(h + 1) * rows, :].astype(F32)
        cols = [pl.ds(pl.multiple_of(c * blk, blk), blk) for c in (ca, cb)]

        def attend(i, carry):
            rs = [ROW_UNROLL * i + t for t in range(ROW_UNROLL)]
            qs = [jnp.concatenate([q_s[r, cs, :] for cs in cols], axis=0) for r in rs]
            qm = [jnp.concatenate([jnp.where(lane_head == h, q, jnp.zeros_like(q)) for h in range(heads)], axis=0) for q in qs]
            sc = [mm(a, kt_s[r]) * scale + bias_f[...] for a, r in zip(qm, rs)]
            pe = [jnp.exp(s - jnp.max(s, axis=-1, keepdims=True)) for s in sc]
            ls = [1.0 / jnp.sum(e, axis=-1, keepdims=True) for e in pe]
            os = [mm(e.astype(BF16), v_s[r]) * l for e, r, l in zip(pe, rs, ls)]
            upds = []
            for r, o in zip(rs, os):
                mix = sum(jnp.where(lane_head == h, o[h * nq:(h + 1) * nq], 0.0) for h in range(heads))
                gate = jnp.concatenate([g_s[r, cs, :] for cs in cols], axis=0)
                upds.append(mm((mix * gate).astype(BF16), wo_s[...]))
            for r, upd in zip(rs, upds):
                for k, c in enumerate((ca, cb)):
                    z1_ref[pl.ds(pl.multiple_of(r * seq + c * blk, blk), blk), :] = (
                        z_ref[r, cols[k], :] + upd[k * blk:(k + 1) * blk])
            return carry

        half = rows // ROW_UNROLL // 2
        lax.fori_loop(0, half, attend, 0)

        @pl.when(p + 1 < chips // 2)
        def _():
            fetch_bias(p + 1)

        lax.fori_loop(half, 2 * half, attend, 0)

        for dev in devs:
            for j in range(rows):
                col = dev * rows + j
                hsend[col] = z1_ref[pl.ds(col, rows, stride=seq), :].astype(BF16)
        for dev in devs:
            @pl.when(dev != me)
            def _():
                h_copy(dev).start()

            @pl.when(dev == me)
            def _():
                ht[:, pl.ds(pl.multiple_of(me * rows, rows), rows), :] = hsend[pl.ds(pl.multiple_of(me * rows, rows), rows)]
        return carry

    def h_copy(dev):
        return remote(hsend.at[pl.ds(dev * rows, rows)], ht.at[:, pl.ds(pl.multiple_of(me * rows, rows), rows), :],
                      h_ss.at[dev], h_rs.at[me], dev)

    def h_wait(src):
        remote(hsend.at[pl.ds(src * rows, rows)], ht.at[:, pl.ds(pl.multiple_of(src * rows, rows), rows), :],
               h_ss.at[src], h_rs.at[src], src).wait_recv()

    lax.fori_loop(0, chips // 2, start_pair, 0)

    pair_bias(lambda r: z1_ref[pl.ds(pl.multiple_of(r * seq, seq), seq), :].astype(BF16).astype(F32), None, wb_e, erecv)
    bias_send(erecv, e_ss, e_rs)
    wide = wp_e[...].astype(F32)
    wt_e[...] = jnp.concatenate([wide[:, :chan], wide[:, 2 * chan:]], axis=1).T.astype(BF16)

    for dist in range(1, chips):
        off = (dist + 1) // 2 if dist % 2 else chips - dist // 2
        c = lax.rem(chip + off, chips)
        bias_wait(erecv, e_ss, e_rs, c * CORES + core)
        forward(erecv, ef_ss, e_rs, c).start()
    for c in range(chips):
        bias_wait(erecv, e_ss, e_rs, c * CORES + (CORES - 1 - core))

    def widen(dev, carry):
        for h in range(heads):
            bias_e[h, pl.ds(pl.multiple_of(dev * rows, rows), rows), :] = erecv[dev, h * rows:(h + 1) * rows, :].astype(F32)
        return carry

    lax.fori_loop(0, n, widen, 0)
    for off in range(1, n):
        h_wait(lax.rem(me + off, n))

    def d_copy(dev, grp):
        src = dsend.at[pl.ds(grp * COL_GROUP, COL_GROUP), pl.ds(pl.multiple_of(dev * rows, rows), rows), :]
        dst = drecv.at[pl.ds(me * rows + grp * COL_GROUP, COL_GROUP)]
        return remote(src, dst, d_ss.at[dev, grp], d_rs.at[me, grp], dev)

    def end_cols(i, carry):
        js = [COL_UNROLL * i + t for t in range(COL_UNROLL)]
        hs = [ht[j] for j in js]
        us = [norm(h.astype(F32)) for h in hs]
        keys = [mm(u, wp_e[:, chan:2 * chan]).astype(BF16) for u in us]
        trs = [mm(wt_e[...], u, 1, 1) for u in us]
        es = []
        for key, tr in zip(keys, trs):
            qt = tr[:chan].astype(BF16)
            vt = tr[chan:2 * chan].astype(BF16)
            gt = sigmoid(tr[2 * chan:])
            parts = []
            for h in range(heads):
                pieces = [jnp.zeros((hd, seq), BF16)] * heads
                pieces[h] = qt[h * hd:(h + 1) * hd]
                s = mm(key, jnp.concatenate(pieces, axis=0)) * scale + bias_e[h]
                e = jnp.exp(s - jnp.max(s, axis=0, keepdims=True))
                l = 1.0 / jnp.sum(e, axis=0, keepdims=True)
                parts.append(mm(vt[h * hd:(h + 1) * hd], e.astype(BF16)) * l)
            og = (jnp.concatenate(parts, axis=0) * gt).astype(BF16)
            es.append(mm(og, wo_e[...], 0, 0))
        z2 = [h.astype(F32) + e for h, e in zip(hs, es)]
        hid = [jnp.maximum(mm(norm(z), w1[...]), 0.0).astype(BF16) for z in z2]
        ts = [mm(x, w2[...]) for x in hid]
        for j, e, t in zip(js, es, ts):
            dsend[j] = (e + t).astype(BF16)
        return carry

    def end_group(grp, carry):
        lax.fori_loop(grp * (COL_GROUP // COL_UNROLL), (grp + 1) * (COL_GROUP // COL_UNROLL), end_cols, 0)
        for off in range(1, n):
            d_copy(lax.rem(me + off, n), grp).start()
        drecv[pl.ds(me * rows + grp * COL_GROUP, COL_GROUP)] = (
            dsend[pl.ds(grp * COL_GROUP, COL_GROUP), pl.ds(pl.multiple_of(me * rows, rows), rows), :])
        return carry

    lax.fori_loop(0, rows // COL_GROUP, end_group, 0)

    bias_drain(brecv, b_ss, b_rs, bf_ss)
    bias_drain(erecv, e_ss, e_rs, ef_ss)
    for off in range(1, n):
        dev = lax.rem(me + off, n)
        h_copy(dev).wait_send()
        for grp in range(rows // COL_GROUP):
            d_copy(dev, grp).wait_send()
            src = dsend.at[pl.ds(grp * COL_GROUP, COL_GROUP), pl.ds(pl.multiple_of(dev * rows, rows), rows), :]
            dst = drecv.at[pl.ds(dev * rows + grp * COL_GROUP, COL_GROUP)]
            remote(src, dst, d_ss.at[dev, grp], d_rs.at[dev, grp], dev).wait_recv()


def solution(mesh):
    row_spec = P(('dp', AXIS), None, None)
    n = mesh.shape[AXIS]

    def local_fn(z, wp_s, wb_s, wo_s, wp_e, wb_e, wo_e, w1, w2):
        rows, seq, chan = z.shape
        heads = wb_s.shape[0]
        hrows = heads * rows
        nq = 2 * CORES * rows
        dma = pltpu.SemaphoreType.DMA
        groups = rows // COL_GROUP
        vmem = pl.BlockSpec(memory_space=pltpu.VMEM)
        z1, delta = pl.pallas_call(
            functools.partial(kernel, n, rows, seq, heads),
            out_shape=(jax.ShapeDtypeStruct((rows * seq, chan), F32), jax.ShapeDtypeStruct((seq, rows, chan), BF16)),
            in_specs=[vmem] * 9,
            out_specs=(vmem, vmem),
            scratch_shapes=[
                pltpu.VMEM((rows, seq, chan), BF16),
                pltpu.VMEM((rows, seq, chan), BF16),
                pltpu.VMEM((rows, chan, seq), BF16),
                pltpu.VMEM((rows, seq, chan), BF16),
                pltpu.VMEM((rows, seq, chan), F32),
                pltpu.VMEM((hrows, seq), F32),
                pltpu.VMEM((n, hrows, seq), BF16),
                pltpu.VMEM((heads * nq, seq), F32),
                pltpu.VMEM((seq, rows, chan), BF16),
                pltpu.VMEM((rows, seq, chan), BF16),
                pltpu.VMEM((n, hrows, seq), BF16),
                pltpu.VMEM((heads, seq, seq), F32),
                pltpu.VMEM((rows, seq, chan), BF16),
                pltpu.VMEM((3 * chan, chan), BF16),
                dma((n,)), dma((n,)), dma((n,)), dma((n,)), dma((n,)), dma((n,)),
                dma((n,)), dma((n,)), dma((n, groups)), dma((n, groups)),
            ],
            compiler_params=pltpu.CompilerParams(collective_id=0, has_side_effects=True),
        )(z, wp_s, wb_s, wo_s, wp_e, wb_e, wo_e, w1, w2)
        return z1.reshape(rows, seq, chan) + jnp.swapaxes(delta, 0, 1).astype(F32)

    return jax.shard_map(local_fn, mesh=mesh, in_specs=(row_spec,) + (P(),) * 8, out_specs=row_spec, check_vma=False)
```

time: 208 us -> 106 us (0.51)
  blocking collectives: 105 us -> 0 us
  Pallas kernels: 0 us -> 101 us
  matrix products: 57.2 us -> 0 us
  local copies, waits for them, and re-layouts: 28.9 us -> 1.96 us
  other arithmetic: 16.5 us -> 3.08 us
    pallas_call x0 -> x1, Pallas kernels: none -> 101 us  [local_fn(): pl.pallas_call(functools.partial(kernel, n, rows, seq, heads), out_shape=...]
    all_to_all x2 -> x0, blocking collectives: 64 us -> none  [the longest x1 33.4 us: local_fn(): delta_rows = lax.all_to_all(delta_cols, 'sp', 0, 1, tiled=True)]
    all_gather x2 -> x0, blocking collectives: 40.7 us -> none  [the longest x1 24.1 us: local_fn(): bias_s = lax.all_gather(bias_loc, 'sp', axis=1, tiled=True)]
    dot_general x9 -> x0, matrix products: 37 us -> none  [the longest x2 16 us: attend(): jnp.einsum(mix_form, attn_prob, val_vecs, preferred_element_type=jnp.floa...]
    sub x2 -> x0, matrix products: 20.2 us -> none  [attend(): attn_prob = jax.nn.softmax(scores, axis=-1).astype(jnp.bfloat16)]
    slice x8 -> x0, local copies, waits for them, and re-layouts: 13 us -> none  [the longest x4 6.76 us: project(): projected[..., channels:2 * channels].astype(jnp.bfloat16)]
    convert_element_type x8 -> x0, local copies, waits for them, and re-layouts: 8.24 us -> none  [the longest x2 4.04 us: attend(): scores = scores * head_dim ** (-0.5) + bias_full.astype(jnp.float32)]
    reduce_sum x5 -> x0, other arithmetic: 5.82 us -> none  [the longest x2 2.97 us: layer_norm(): mean_c = jnp.mean(vals_f, axis=-1, keepdims=True)]
where the time goes in v1:
time: 106 us
  Pallas kernels  101 us (95%)
  other arithmetic  3.08 us (3%)
  local copies, waits for them, and re-layouts  1.96 us (2%)
    pallas_call x1, Pallas kernels, local_fn(): pl.pallas_call(functools.partial(kernel, n, rows, seq, heads), out_shape=...  101 us
    add x1, other arithmetic, local_fn(): return z1.reshape(rows, seq, chan) + jnp.swapaxes(delta, 0, 1).astype(F32)  3.08 us

profile of v1, /device:TPU:21, one launch (start us, length us, event | category | flops | bytes accessed | tf_op | source)
XLA Modules:
  0.0 105.8 jit_solution(9858847487163309631)
XLA Ops:
  0.0 100.7 %shard_map.91 = (f32[4096,128]{1,0:T(8,128)}, bf16[256,16,128]{2,1,0:T(8,128)(2,1)}) custom-call(f32[16,256,128]{2,1,0:T(8,128)} %z_ref.1, bf16[128,512]{1,0:T(8,128)(2,1)} %wp_s.1, bf16[4,128]{1,0:T(4,128)(2,1)} %wb_s.1, bf16[128,128]{1,0:T(8,128)(2,1)} %wo_s.1, bf16[128,512]{1,0:T(8,128)(2,1)} %wp_e.1, bf16[4,128]{1,0:T(4,128)(2,1)} %wb_e.1, ...), custom_call_target="tpu_custom_call" | custom-call | tf_op jit(solution)/shard_map/pallas_call | solution.py:294
  100.7 3.1 %bitcast_add_fusion = f32[16,256,128]{2,0,1:T(8,128)S(1)} fusion(f32[16,256,128]{2,1,0:T(8,128)} %bitcast.3, bf16[256,16,128]{2,1,0:T(8,128)(2,1)} %get-tuple-element.8), kind=kLoop, calls=%fused_computation | loop fusion | flops 1048576 | bytes 5242880 | tf_op jit(solution)/shard_map/add | solution.py:319
  103.8 2.0 %copy.12 = f32[16,256,128]{2,1,0:T(8,128)} copy(f32[16,256,128]{2,0,1:T(8,128)S(1)} %bitcast_add_fusion) | data formatting | bytes 4194304 | tf_op jit(solution)/shard_map/add | solution.py:319

commit v2 on v1

v2 whole, which is shorter than its diff:
```python
import functools

import jax
import jax.numpy as jnp
from jax import lax
from jax.experimental import pallas as pl
from jax.experimental.pallas import tpu as pltpu
from jax.sharding import PartitionSpec as P

LN_EPS = 1e-5
F32, BF16 = jnp.float32, jnp.bfloat16
MESH = pl.DeviceIdType.MESH
AXIS = "sp"
CORES = 2
HALVES = 2
GROUPS = 2
ROW_UNROLL = 8
COL_UNROLL = 2
LN_UNROLL = 4
PAD = 8


def norm(vals):
    mean_c = jnp.mean(vals, axis=-1, keepdims=True)
    centered = vals - mean_c
    variance = jnp.mean(centered * centered, axis=-1, keepdims=True)
    return (centered * lax.rsqrt(variance + LN_EPS)).astype(BF16)


def mm(a, b, ca=1, cb=0):
    return lax.dot_general(a, b, (((ca,), (cb,)), ((), ())), preferred_element_type=F32)


def sigmoid(x):
    return 1.0 / (1.0 + jnp.exp(-x))


def kernel(n, rows, seq, heads, z_hbm, wps_h, wbs_h, wos_h, wpe_h, wbe_h, woe_h, w1_h, w2_h,
           z1_ref, drecv,
           z_ref, wp_s, wb_s, wo_s, wp_e, wb_e, wo_e, w1, w2,
           u_s, q_s, kt_s, v_s, g_s, bacc, brecv, bias_all, bias_f, zb, hsend, ht, erecv, bias_e, stage, dsend, wk_s, wk_e,
           z_sem, w_sem, b_ss, b_rs, bf_ss, e_ss, e_rs, ef_ss, h_ss, h_rs, d_ss, d_rs):
    chan = wo_s.shape[0]
    hd = chan // heads
    scale = hd ** -0.5
    chips = n // CORES
    part = rows // HALVES
    me = lax.axis_index(AXIS)
    chip, core = me // CORES, lax.rem(me, CORES)
    other = CORES - 1 - core
    partner = chip * CORES + other
    hrows = heads * rows

    def remote(src, dst, ss, rs, dev):
        return pltpu.make_async_remote_copy(src_ref=src, dst_ref=dst, send_sem=ss, recv_sem=rs,
                                            device_id={AXIS: dev}, device_id_type=MESH)

    def aligned(i, k):
        return pl.multiple_of(i, k)

    barrier = pltpu.get_barrier_semaphore()
    for off in range(1, n):
        pl.semaphore_signal(barrier, 1, device_id={AXIS: lax.rem(me + off, n)}, device_id_type=MESH)

    def z_load(i):
        sl = pl.ds(i * LN_UNROLL, LN_UNROLL)
        return pltpu.make_async_copy(z_hbm.at[sl], z_ref.at[sl], z_sem.at[i])

    w_loads = [pltpu.make_async_copy(src, dst, w_sem.at[i]) for i, (src, dst) in enumerate(
        [(wbs_h, wb_s), (wps_h, wp_s), (wos_h, wo_s), (wbe_h, wb_e), (wpe_h, wp_e), (woe_h, wo_e), (w1_h, w1), (w2_h, w2)])]
    w_loads[0].start()
    for i in range(rows // LN_UNROLL):
        z_load(i).start()
    for cp in w_loads[1:]:
        cp.start()

    row_of = lax.rem(lax.broadcasted_iota(jnp.int32, (hrows, chan), 0), rows)
    lane_head = lax.broadcasted_iota(jnp.int32, (1, chan), 1) // hd

    def pair_bias(ready, get_row, put_row, wb, out):
        wide = wb[...].astype(F32)
        wide = jnp.concatenate([jnp.broadcast_to(wide[h:h + 1], (rows, chan)) for h in range(heads)], axis=0)
        bacc[...] = jnp.zeros_like(bacc)

        def step(i, carry):
            ready(i)
            rs = [LN_UNROLL * i + t for t in range(LN_UNROLL)]
            us = [norm(get_row(r)) for r in rs]
            total = sum(mm(jnp.where(row_of == r, wide, 0.0).astype(BF16), u, 1, 1) for r, u in zip(rs, us))
            if put_row is not None:
                for r, u in zip(rs, us):
                    put_row(r, u)
            bacc[...] += total
            return carry

        lax.fori_loop(0, rows // LN_UNROLL, step, 0)
        out[me] = bacc[...].astype(BF16)

    def bias_copy(buf, ss, rs, dev):
        return remote(buf.at[me], buf.at[me], ss.at[dev], rs.at[me], dev)

    def by_distance(dist):
        return lax.rem(chip + ((dist + 1) // 2 if dist % 2 else chips - dist // 2), chips)

    def bias_send(buf, ss, rs):
        bias_copy(buf, ss, rs, partner).start()
        for dist in range(1, chips):
            bias_copy(buf, ss, rs, by_distance(dist) * CORES + core).start()

    def bias_wait(buf, ss, rs, src):
        remote(buf.at[src], buf.at[src], ss.at[src], rs.at[src], partner).wait_recv()

    def forward(buf, ss, rs, c):
        src = c * CORES + core
        return remote(buf.at[src], buf.at[src], ss.at[c], rs.at[src], partner)

    def bias_drain(buf, ss, rs, fss):
        bias_copy(buf, ss, rs, partner).wait_send()
        for dist in range(1, chips):
            c = by_distance(dist)
            bias_copy(buf, ss, rs, c * CORES + core).wait_send()
            forward(buf, fss, rs, c).wait_send()

    def put_u(r, u):
        u_s[r] = u

    w_loads[0].wait()
    with jax.named_scope("bias_rows"):
        pair_bias(lambda i: z_load(i).wait(), lambda r: z_ref[r], put_u, wb_s, brecv)
    with jax.named_scope("barrier"):
        pl.semaphore_wait(barrier, n - 1)
    bias_send(brecv, b_ss, b_rs)
    for cp in w_loads[1:]:
        cp.wait()

    wk_s[...] = wp_s[:, chan:2 * chan].astype(F32).T.astype(BF16)
    wk_e[...] = wp_e[:, chan:2 * chan].astype(F32).T.astype(BF16)

    def by_part(x):
        return jnp.concatenate([x[d * rows + hf * part:d * rows + (hf + 1) * part] for hf in range(HALVES) for d in range(n)], axis=0)

    def project(i, carry):
        for t in range(2):
            r = 2 * i + t
            u = u_s[r]
            pr = mm(u, wp_s[...])
            q_s[r] = by_part(pr[:, :chan]).astype(BF16)
            kt_s[r] = mm(wk_s[...], u, 1, 1).astype(BF16)
            v_s[r] = pr[:, 2 * chan:3 * chan].astype(BF16)
            g_s[r] = by_part(sigmoid(pr[:, 3 * chan:]))
        return carry

    with jax.named_scope("project"):
        lax.fori_loop(0, rows // 2, project, 0)

    gchips = chips // GROUPS
    nq = gchips * CORES * part

    def chips_of(g):
        offs = (chips - 2 * g, 1 + 2 * g, chips - 1 - 2 * g, 2 + 2 * g)
        return [lax.rem(chip + off, chips) for off in offs]

    def fetch_bias(g):
        for c in chips_of(g):
            @pl.when(c != chip)
            def _():
                bias_wait(brecv, b_ss, b_rs, c * CORES + core)
                forward(brecv, bf_ss, b_rs, c).start()

    def attention(qs, kts, vs, biases, gates, wo):
        nrow = qs[0].shape[0]
        qm = [jnp.concatenate([jnp.where(lane_head == h, q, jnp.zeros_like(q)) for h in range(heads)], axis=0) for q in qs]
        sc = [mm(a, kt) * scale + b[...] for a, kt, b in zip(qm, kts, biases)]
        pe = [jnp.exp(s - jnp.max(s, axis=-1, keepdims=True)) for s in sc]
        ls = [1.0 / jnp.sum(e, axis=-1, keepdims=True) for e in pe]
        os = [mm(e.astype(BF16), v) * l for e, v, l in zip(pe, vs, ls)]
        upds = []
        for o, gate in zip(os, gates):
            mix = sum(jnp.where(lane_head == h, o[h * nrow:(h + 1) * nrow], 0.0) for h in range(heads))
            upds.append(mm((mix * gate).astype(BF16), wo[...]))
        return upds

    def h_copy(dev, hf):
        return remote(hsend.at[pl.ds(dev * rows + hf * part, part)],
                      ht.at[pl.ds(hf * part, part), pl.ds(aligned(me * rows, rows), rows), :],
                      h_ss.at[dev, hf], h_rs.at[me, hf], dev)

    def h_wait(src, hf):
        remote(hsend.at[pl.ds(src * rows + hf * part, part)],
               ht.at[pl.ds(hf * part, part), pl.ds(aligned(src * rows, rows), rows), :],
               h_ss.at[src, hf], h_rs.at[src, hf], src).wait_recv()

    with jax.named_scope("fetch_first"):
        fetch_bias(0)

    def start_block(b, carry):
        hf, g = b // GROUPS, lax.rem(b, GROUPS)
        cs = chips_of(g)
        devs = [c * CORES + s for c in cs for s in range(CORES)]

        @pl.when(hf == 0)
        def _():
            with jax.named_scope("wait_block"):
                for c in cs:
                    bias_wait_other(c)
            for dev in devs:
                bias_all[dev] = brecv[dev].astype(F32)

        for h in range(heads):
            for k, dev in enumerate(devs):
                bias_f[h * nq + k * part:h * nq + (k + 1) * part, :] = bias_all[dev, pl.ds(aligned(h * rows + hf * part, part), part), :]
        wide = CORES * part
        qcols = [pl.ds(aligned((hf * chips + c) * wide, wide), wide) for c in cs]
        zcols = [aligned(dev * rows + hf * part, part) for dev in devs]

        def attend(i, carry):
            rs = [ROW_UNROLL * i + t for t in range(ROW_UNROLL)]
            qs = [jnp.concatenate([q_s[r, sl, :] for sl in qcols], axis=0) for r in rs]
            gates = [jnp.concatenate([g_s[r, sl, :] for sl in qcols], axis=0) for r in rs]
            upds = attention(qs, [kt_s[r] for r in rs], [v_s[r] for r in rs], [bias_f] * len(rs), gates, wo_s)
            for r, upd in zip(rs, upds):
                z1 = jnp.concatenate([z_ref[r, pl.ds(zc, part), :] for zc in zcols], axis=0) + upd
                for k, zc in enumerate(zcols):
                    z1_ref[pl.ds(aligned(r * seq + zc, part), part), :] = z1[k * part:(k + 1) * part]
                zb[pl.ds(aligned(r * (nq + PAD), PAD), nq), :] = z1
            return carry

        half = rows // ROW_UNROLL // 2
        with jax.named_scope("attend_a"):
            lax.fori_loop(0, half, attend, 0)
        with jax.named_scope("fetch_next"):
            @pl.when(b == 0)
            def _():
                fetch_bias(1)
        with jax.named_scope("attend_b"):
            lax.fori_loop(half, 2 * half, attend, 0)

        for k, dev in enumerate(devs):
            for j in range(part):
                hsend[dev * rows + hf * part + j] = zb[pl.ds(k * part + j, rows, stride=nq + PAD), :].astype(BF16)
        for dev in devs:
            @pl.when(jnp.logical_and(dev != me, hf == 0))
            def _():
                h_copy(dev, hf).start()
        return carry

    def bias_wait_other(c):
        bias_wait(brecv, b_ss, b_rs, c * CORES + other)

    lax.fori_loop(0, HALVES * GROUPS, start_block, 0)

    with jax.named_scope("bias_cols"):
        pair_bias(lambda i: None, lambda r: z1_ref[pl.ds(aligned(r * seq, seq), seq), :].astype(BF16).astype(F32), None, wb_e, erecv)
    bias_send(erecv, e_ss, e_rs)
    for hf in range(1, HALVES):
        for off in range(1, n):
            h_copy(lax.rem(me + off, n), hf).start()
    ht[:, pl.ds(aligned(me * rows, rows), rows), :] = hsend[pl.ds(aligned(me * rows, rows), rows)]

    with jax.named_scope("wait_cols"):
        for dist in range(1, chips):
            c = by_distance(dist)
            bias_wait(erecv, e_ss, e_rs, c * CORES + core)
            forward(erecv, ef_ss, e_rs, c).start()
        for c in range(chips):
            bias_wait(erecv, e_ss, e_rs, c * CORES + other)

    def widen(h, carry):
        tall = jnp.concatenate([erecv[dev, pl.ds(aligned(h * rows, rows), rows), :] for dev in range(n)], axis=0)
        bias_e[pl.ds(aligned(h * seq, seq), seq), :] = tall.astype(F32).T
        return carry

    with jax.named_scope("widen"):
        lax.fori_loop(0, heads, widen, 0)

    def d_copy(dev, hf):
        return remote(dsend.at[hf, pl.ds(dev * rows, rows)], drecv.at[:, me, hf], d_ss.at[dev, hf], d_rs.at[me, hf], dev)

    def end_cols(hf, i, carry):
        js = [COL_UNROLL * i + t for t in range(COL_UNROLL)]
        hs = [ht[hf * part + j] for j in js]
        us = [norm(h.astype(F32)) for h in hs]
        prs = [mm(u, wp_e[...]) for u in us]
        kts = [mm(wk_e[...], u, 1, 1).astype(BF16) for u in us]
        es = attention([p[:, :chan].astype(BF16) for p in prs], kts, [p[:, 2 * chan:3 * chan].astype(BF16) for p in prs],
                       [bias_e] * len(js), [sigmoid(p[:, 3 * chan:]) for p in prs], wo_e)
        z2 = [h.astype(F32) + e for h, e in zip(hs, es)]
        hid = [jnp.maximum(mm(norm(z), w1[...]), 0.0).astype(BF16) for z in z2]
        ts = [mm(x, w2[...]) for x in hid]
        for j, e, t in zip(js, es, ts):
            stage[pl.ds(aligned(j * (seq + PAD), PAD), seq), :] = e + t
        return carry

    for hf in range(HALVES):
        with jax.named_scope("wait_h"):
            for off in range(1, n):
                h_wait(lax.rem(me + off, n), hf)
        with jax.named_scope("end_cols"):
            lax.fori_loop(0, part // COL_UNROLL, functools.partial(end_cols, hf), 0)

        def pack(dev, carry):
            for t in range(rows):
                i = dev * rows + t
                dsend[hf, i] = stage[pl.ds(i, part, stride=seq + PAD), :].astype(BF16)
            return carry

        with jax.named_scope("pack"):
            lax.fori_loop(0, n, pack, 0)
        for off in range(1, n):
            d_copy(lax.rem(me + off, n), hf).start()
        drecv[:, me, hf] = dsend[hf, pl.ds(me * rows, rows)]

    with jax.named_scope("drain"):
        bias_drain(brecv, b_ss, b_rs, bf_ss)
        bias_drain(erecv, e_ss, e_rs, ef_ss)
        for off in range(1, n):
            dev = lax.rem(me + off, n)
            for hf in range(HALVES):
                h_copy(dev, hf).wait_send()
                d_copy(dev, hf).wait_send()
                remote(dsend.at[hf, pl.ds(dev * rows, rows)], drecv.at[:, dev, hf], d_ss.at[dev, hf], d_rs.at[dev, hf], dev).wait_recv()


def solution(mesh):
    row_spec = P(('dp', AXIS), None, None)
    n = mesh.shape[AXIS]

    def local_fn(z, *weights):
        rows, seq, chan = z.shape
        heads = weights[1].shape[0]
        hrows = heads * rows
        part = rows // HALVES
        nq = n // GROUPS * part
        dma = pltpu.SemaphoreType.DMA
        vmem = pl.BlockSpec(memory_space=pltpu.VMEM)
        z1, delta = pl.pallas_call(
            functools.partial(kernel, n, rows, seq, heads),
            out_shape=(jax.ShapeDtypeStruct((rows * seq, chan), F32), jax.ShapeDtypeStruct((rows, n, HALVES, part, chan), BF16)),
            in_specs=[pl.BlockSpec(memory_space=pltpu.HBM)] * 9,
            out_specs=(vmem, vmem),
            scratch_shapes=[pltpu.VMEM(z.shape, z.dtype)] + [pltpu.VMEM(w.shape, w.dtype) for w in weights] + [
                pltpu.VMEM((rows, seq, chan), BF16),
                pltpu.VMEM((rows, seq, chan), BF16),
                pltpu.VMEM((rows, chan, seq), BF16),
                pltpu.VMEM((rows, seq, chan), BF16),
                pltpu.VMEM((rows, seq, chan), F32),
                pltpu.VMEM((hrows, seq), F32),
                pltpu.VMEM((n, hrows, seq), BF16),
                pltpu.VMEM((n, hrows, seq), F32),
                pltpu.VMEM((heads * nq, seq), F32),
                pltpu.VMEM((rows * (nq + PAD), chan), F32),
                pltpu.VMEM((seq, rows, chan), BF16),
                pltpu.VMEM((rows, seq, chan), BF16),
                pltpu.VMEM((n, hrows, seq), BF16),
                pltpu.VMEM((heads * seq, seq), F32),
                pltpu.VMEM((part * (seq + PAD), chan), F32),
                pltpu.VMEM((HALVES, seq, part, chan), BF16),
                pltpu.VMEM((chan, chan), BF16),
                pltpu.VMEM((chan, chan), BF16),
                dma((rows // LN_UNROLL,)), dma((len(weights),)),
                dma((n,)), dma((n,)), dma((n,)), dma((n,)), dma((n,)), dma((n,)),
                dma((n, HALVES)), dma((n, HALVES)), dma((n, HALVES)), dma((n, HALVES)),
            ],
            compiler_params=pltpu.CompilerParams(collective_id=0, has_side_effects=True, vmem_limit_bytes=40 * 2 ** 20),
        )(*[pltpu.with_memory_space_constraint(a, pltpu.HBM) for a in (z,) + weights])
        return z1.reshape(rows, seq, chan) + delta.reshape(rows, seq, chan).astype(F32)

    return jax.shard_map(local_fn, mesh=mesh, in_specs=(row_spec,) + (P(),) * 8, out_specs=row_spec, check_vma=False)
```

time: 106 us -> 82.9 us (0.78)
  Pallas kernels: 101 us -> 81.2 us
  local copies, waits for them, and re-layouts: 1.96 us -> 0 us
  other arithmetic: 3.08 us -> 1.61 us
    pallas_call x1, Pallas kernels: 101 us -> 81.2 us  [local_fn(): pl.pallas_call(functools.partial(kernel, n, rows, seq, heads), out_shape=...]
    add x1 -> x0, local copies, waits for them, and re-layouts: 1.96 us -> none  [local_fn(): return z1.reshape(rows, seq, chan) + jnp.swapaxes(delta, 0, 1).astype(F32)]
    add x1, other arithmetic: 3.08 us -> 1.61 us  [local_fn(): z1.reshape(rows, seq, chan) + delta.reshape(rows, seq, chan).astype(F32)]
where the time goes in v2:
time: 82.9 us; the launch traced here: 82.8 us
  Pallas kernels  81.2 us (98%)
  other arithmetic  1.61 us (2%)
    pallas_call x1, Pallas kernels, local_fn(): pl.pallas_call(functools.partial(kernel, n, rows, seq, heads), out_shape=...  81.2 us

profile of v2, /device:TPU:21, one launch (start us, length us, event | category | flops | bytes accessed | tf_op | source)
XLA Modules:
  0.0 82.8 jit_solution(9189604693509328315)
XLA Ops:
  0.0 81.2 %shard_map.91 = (f32[4096,128]{1,0:T(8,128)S(1)}, bf16[16,16,2,8,128]{4,3,2,1,0:T(8,128)(2,1)S(1)}) custom-call(f32[16,256,128]{2,1,0:T(8,128)} %z_hbm.1, bf16[128,512]{1,0:T(8,128)(2,1)} %wps_h.1, bf16[4,128]{1,0:T(4,128)(2,1)} %wbs_h.1, bf16[128,128]{1,0:T(8,128)(2,1)} %wos_h.1, bf16[128,512]{1,0:T(8,128)(2,1)} %wpe_h.1, bf16[4,128]{1,0:T(4,128)(2,1)} %wbe_h.1, ...), custom_call_target="tpu_custom_call" | custom-call | tf_op jit(solution)/shard_map/pallas_call | solution.py:336
  81.2 1.6 %convert_add_fusion = f32[16,256,128]{2,1,0:T(8,128)} fusion(f32[16,256,128]{2,1,0:T(8,128)S(1)} %bitcast.4, bf16[16,16,2,8,128]{4,3,2,1,0:T(8,128)(2,1)S(1)} %get-tuple-element.8), kind=kLoop, calls=%fused_computation | loop fusion | flops 1048576 | bytes 5242880 | tf_op jit(solution)/shard_map/add | solution.py:366

commit v3 on v2

v3 whole, which is shorter than its diff:
```python
import functools

import jax
import jax.numpy as jnp
from jax import lax
from jax.experimental import pallas as pl
from jax.experimental.pallas import tpu as pltpu
from jax.sharding import PartitionSpec as P

LN_EPS = 1e-5
F32, BF16 = jnp.float32, jnp.bfloat16
MESH = pl.DeviceIdType.MESH
AXIS = "sp"
CORES = 2
HALVES = 2
COL_GROUP = 4
HOLD_FROM = 2
ROW_UNROLL = 8
COL_UNROLL = 2
LN_UNROLL = 4
PAD = 8


def norm(vals):
    mean_c = jnp.mean(vals, axis=-1, keepdims=True)
    centered = vals - mean_c
    variance = jnp.mean(centered * centered, axis=-1, keepdims=True)
    return (centered * lax.rsqrt(variance + LN_EPS)).astype(BF16)


def mm(a, b, ca=1, cb=0):
    return lax.dot_general(a, b, (((ca,), (cb,)), ((), ())), preferred_element_type=F32)


def sigmoid(x):
    return 1.0 / (1.0 + jnp.exp(-x))


def kernel(n, rows, seq, heads, z_hbm, wps_h, wbs_h, wos_h, wpe_h, wbe_h, woe_h, w1_h, w2_h,
           z1_ref,
           z_ref, wp_s, wb_s, wo_s, wp_e, wb_e, wo_e, w1, w2,
           u_s, q_s, kt_s, v_s, g_s, bacc, brecv, bias_f, zb, hsend, ht, erecv, bias_e, dsend, drecv, tmp,
           z_sem, w_sem, b_ss, b_rs, e_ss, e_rs, h_ss, h_rs, d_ss, d_rs):
    chan = wo_s.shape[0]
    hd = chan // heads
    scale = hd ** -0.5
    chips = n // CORES
    part = rows // HALVES
    me = lax.axis_index(AXIS)
    chip, core = me // CORES, lax.rem(me, CORES)
    other = CORES - 1 - core
    partner = chip * CORES + other
    hrows = heads * rows

    def remote(src, dst, ss, rs, dev):
        return pltpu.make_async_remote_copy(src_ref=src, dst_ref=dst, send_sem=ss, recv_sem=rs,
                                            device_id={AXIS: dev}, device_id_type=MESH)

    def aligned(i, k):
        return pl.multiple_of(i, k)

    barrier = pltpu.get_barrier_semaphore()
    for off in range(1, n):
        pl.semaphore_signal(barrier, 1, device_id={AXIS: lax.rem(me + off, n)}, device_id_type=MESH)

    def z_load(i):
        sl = pl.ds(i * LN_UNROLL, LN_UNROLL)
        return pltpu.make_async_copy(z_hbm.at[sl], z_ref.at[sl], z_sem.at[i])

    w_loads = [pltpu.make_async_copy(src, dst, w_sem.at[i]) for i, (src, dst) in enumerate(
        [(wbs_h, wb_s), (wps_h, wp_s), (wos_h, wo_s), (wbe_h, wb_e), (wpe_h, wp_e), (woe_h, wo_e), (w1_h, w1), (w2_h, w2)])]
    w_loads[0].start()
    for i in range(rows // LN_UNROLL):
        z_load(i).start()
    for cp in w_loads[1:]:
        cp.start()

    row_of = lax.rem(lax.broadcasted_iota(jnp.int32, (hrows, chan), 0), rows)
    lane_head = lax.broadcasted_iota(jnp.int32, (1, chan), 1) // hd

    def pair_bias(ready, get_row, put_row, wb, out):
        wide = wb[...].astype(F32)
        wide = jnp.concatenate([jnp.broadcast_to(wide[h:h + 1], (rows, chan)) for h in range(heads)], axis=0)
        bacc[...] = jnp.zeros_like(bacc)

        def step(i, carry):
            ready(i)
            rs = [LN_UNROLL * i + t for t in range(LN_UNROLL)]
            us = [norm(get_row(r)) for r in rs]
            total = sum(mm(jnp.where(row_of == r, wide, 0.0).astype(BF16), u, 1, 1) for r, u in zip(rs, us))
            if put_row is not None:
                for r, u in zip(rs, us):
                    put_row(r, u)
            bacc[...] += total
            return carry

        lax.fori_loop(0, rows // LN_UNROLL, step, 0)
        out[me] = bacc[...].astype(BF16)

    def bias_copy(buf, ss, rs, dev):
        return remote(buf.at[me], buf.at[me], ss, rs.at[me], dev)

    def by_distance(dist):
        return lax.rem(chip + ((dist + 1) // 2 if dist % 2 else chips - dist // 2), chips)

    def at(off):
        return lax.rem(chip + off + chips, chips)

    def bias_send(buf, ss, rs):
        bias_copy(buf, ss, rs, partner).start()
        for dist in range(1, chips):
            bias_copy(buf, ss, rs, by_distance(dist) * CORES + core).start()

    def bias_wait(buf, ss, rs, src):
        remote(buf.at[src], buf.at[src], ss, rs.at[src], partner).wait_recv()

    def forward(buf, ss, rs, c):
        src = c * CORES + core
        return remote(buf.at[src], buf.at[src], ss, rs.at[src], partner)

    def fetch(buf, ss, rs, c):
        bias_wait(buf, ss, rs, c * CORES + core)
        forward(buf, ss, rs, c).start()

    def sent(buf, ss, rs):
        remote(buf, buf, ss, rs, partner).wait_send()

    def put_u(r, u):
        u_s[r] = u

    w_loads[0].wait()
    with jax.named_scope("bias_rows"):
        pair_bias(lambda i: z_load(i).wait(), lambda r: z_ref[r], put_u, wb_s, brecv)
    with jax.named_scope("barrier"):
        pl.semaphore_wait(barrier, n - 1)
    bias_send(brecv, b_ss, b_rs)
    for cp in w_loads[1:]:
        cp.wait()


    def project(i, carry):
        for t in range(2):
            r = 2 * i + t
            u = u_s[r]
            pr = mm(u, wp_s[...])
            q_s[r] = pr[:, :chan].astype(BF16)
            kt_s[r] = pr[:, chan:2 * chan].T.astype(BF16)
            v_s[r] = pr[:, 2 * chan:3 * chan].astype(BF16)
            g_s[r] = sigmoid(pr[:, 3 * chan:])
        return carry

    with jax.named_scope("project"):
        lax.fori_loop(0, rows // 2, project, 0)

    def attention(qs, kts, vs, biases, gates, wo):
        nrow = qs[0].shape[0]
        qm = [jnp.concatenate([jnp.where(lane_head == h, q, jnp.zeros_like(q)) for h in range(heads)], axis=0) for q in qs]
        sc = [mm(a, kt) * scale + b[...] for a, kt, b in zip(qm, kts, biases)]
        pe = [jnp.exp(s - jnp.max(s, axis=-1, keepdims=True)) for s in sc]
        ls = [1.0 / jnp.sum(e, axis=-1, keepdims=True) for e in pe]
        os = [mm(e.astype(BF16), v) * l for e, v, l in zip(pe, vs, ls)]
        upds = []
        for o, gate in zip(os, gates):
            mix = sum(jnp.where(lane_head == h, o[h * nrow:(h + 1) * nrow], 0.0) for h in range(heads))
            upds.append(mm((mix * gate).astype(BF16), wo[...]))
        return upds

    def h_copy(dev, hf):
        return remote(hsend.at[pl.ds(dev * rows + hf * part, part)],
                      ht.at[pl.ds(hf * part, part), pl.ds(aligned(me * rows, rows), rows), :], h_ss, h_rs.at[hf], dev)

    wide = CORES * rows

    def start_block(cs, between):
        nc = len(cs)
        nq = nc * wide
        for h in range(heads):
            for k in range(nc * CORES):
                src = brecv[cs[k // CORES] * CORES + k % CORES, h * rows:(h + 1) * rows, :]
                bias_f[h * nq + k * rows:h * nq + (k + 1) * rows, :] = src.astype(F32)
        cols = [pl.ds(aligned(c * wide, wide), wide) for c in cs]
        bias = bias_f.at[pl.ds(0, heads * nq)]

        def attend(i, carry):
            rs = [ROW_UNROLL * i + t for t in range(ROW_UNROLL)]
            qs = [jnp.concatenate([q_s[r, sl, :] for sl in cols], axis=0) for r in rs]
            gates = [jnp.concatenate([g_s[r, sl, :] for sl in cols], axis=0) for r in rs]
            upds = attention(qs, [kt_s[r] for r in rs], [v_s[r] for r in rs], [bias] * len(rs), gates, wo_s)
            for r, upd in zip(rs, upds):
                z1 = jnp.concatenate([z_ref[r, sl, :] for sl in cols], axis=0) + upd
                for k, c in enumerate(cs):
                    z1_ref[pl.ds(aligned(r * seq + c * wide, wide), wide), :] = z1[k * wide:(k + 1) * wide]
                zb[pl.ds(aligned(r * (nq + PAD), PAD), nq), :] = z1
            return carry

        half = rows // ROW_UNROLL // 2
        with jax.named_scope("attend_a"):
            lax.fori_loop(0, half, attend, 0)
        with jax.named_scope("fetch_next"):
            between()
        with jax.named_scope("attend_b"):
            lax.fori_loop(half, 2 * half, attend, 0)
        for k, c in enumerate(cs):
            for j in range(wide):
                hsend[c * wide + j] = zb[pl.ds(k * wide + j, rows, stride=nq + PAD), :].astype(BF16)

    def wait_other(c):
        with jax.named_scope("wait_block"):
            bias_wait(brecv, b_ss, b_rs, c * CORES + other)

    def fetch_ring(dist):
        fetch(brecv, b_ss, b_rs, at(dist))
        if isinstance(dist, int):
            if 2 * dist % chips:
                fetch(brecv, b_ss, b_rs, at(-dist))
        else:
            @pl.when(2 * dist < chips)
            def _():
                fetch(brecv, b_ss, b_rs, at(-dist))

    def send_ring(cs, hf):
        for s in range(CORES):
            for c in cs:
                h_copy(c * CORES + s, hf).start()

    bias_wait(brecv, b_ss, b_rs, partner)
    start_block([chip], lambda: fetch_ring(1))
    for hf in range(HALVES):
        h_copy(partner, hf).start()

    def start_ring(dist, carry):
        cs = [at(dist), at(-dist)]
        for c in cs:
            wait_other(c)
        start_block(cs, lambda: fetch_ring(dist + 1))
        send_ring(cs, 0)
        for hf in range(1, HALVES):
            @pl.when(dist < HOLD_FROM)
            def _():
                send_ring(cs, hf)
        return carry

    far = chips // 2
    lax.fori_loop(1, far, start_ring, 0)
    wait_other(at(far))
    start_block([at(far)], lambda: None)
    send_ring([at(far)], 0)

    with jax.named_scope("bias_cols"):
        pair_bias(lambda i: None, lambda r: z1_ref[pl.ds(aligned(r * seq, seq), seq), :].astype(BF16).astype(F32), None, wb_e, erecv)
    bias_send(erecv, e_ss, e_rs)
    for hf in range(1, HALVES):
        for dist in range(HOLD_FROM, far):
            send_ring([at(dist), at(-dist)], hf)
        send_ring([at(far)], hf)
    ht[:, pl.ds(aligned(me * rows, rows), rows), :] = hsend[pl.ds(aligned(me * rows, rows), rows)]

    with jax.named_scope("wait_cols"):
        for dist in range(1, chips):
            fetch(erecv, e_ss, e_rs, by_distance(dist))
        for c in range(chips):
            bias_wait(erecv, e_ss, e_rs, c * CORES + other)

    def widen(h, carry):
        tall = jnp.concatenate([erecv[dev, pl.ds(aligned(h * rows, rows), rows), :] for dev in range(n)], axis=0)
        bias_e[pl.ds(aligned(h * seq, seq), seq), :] = tall.astype(F32).T
        return carry

    with jax.named_scope("widen"):
        lax.fori_loop(0, heads, widen, 0)

    def is_far(off):
        return int(min(off // CORES, chips - off // CORES) > 2)

    def d_copy(off, grp):
        dev = lax.rem(me // CORES * CORES + off // CORES * CORES, n) + (core if off % CORES == 0 else other)
        return remote(dsend.at[pl.ds(grp * COL_GROUP, COL_GROUP), pl.ds(aligned(dev * rows, rows), rows), :],
                      drecv.at[pl.ds(me * rows + grp * COL_GROUP, COL_GROUP)],
                      d_ss, d_rs.at[grp // (part // COL_GROUP), is_far(off)], dev)

    def end_cols(i, carry):
        js = [COL_UNROLL * i + t for t in range(COL_UNROLL)]
        hs = [ht[j] for j in js]
        us = [norm(h.astype(F32)) for h in hs]
        prs = [mm(u, wp_e[...]) for u in us]
        kts = [p[:, chan:2 * chan].T.astype(BF16) for p in prs]
        es = attention([p[:, :chan].astype(BF16) for p in prs], kts, [p[:, 2 * chan:3 * chan].astype(BF16) for p in prs],
                       [bias_e] * len(js), [sigmoid(p[:, 3 * chan:]) for p in prs], wo_e)
        z2 = [h.astype(F32) + e for h, e in zip(hs, es)]
        hid = [jnp.maximum(mm(norm(z), w1[...]), 0.0).astype(BF16) for z in z2]
        ts = [mm(x, w2[...]) for x in hid]
        for j, e, t in zip(js, es, ts):
            dsend[j] = (e + t).astype(BF16)
        return carry

    far_first = sorted(range(1, n), key=lambda off: -min(off // CORES, chips - off // CORES))
    per = COL_GROUP // COL_UNROLL

    def end_group(grp, carry):
        for hf in range(HALVES):
            @pl.when(grp == hf * (part // COL_GROUP))
            def _():
                with jax.named_scope("wait_h"):
                    whole = hsend.at[pl.ds(0, (n - 1) * part)]
                    remote(whole, whole, h_ss, h_rs.at[hf], partner).wait_recv()
        with jax.named_scope("end_cols"):
            lax.fori_loop(grp * per, (grp + 1) * per, end_cols, 0)
        for off in far_first:
            d_copy(off, grp).start()
        return carry

    lax.fori_loop(0, rows // COL_GROUP, end_group, 0)
    drecv[pl.ds(me * rows, rows)] = dsend[:, pl.ds(aligned(me * rows, rows), rows), :]

    pitch = rows + PAD
    with jax.named_scope("finish"):
        for hf in range(HALVES):
            def finish(first, k, carry):
                dev = at(first + k // CORES) * CORES + lax.rem(k, CORES)
                base = dev * (part * pitch)
                for t in range(part):
                    tmp[pl.ds(aligned(base + t * pitch, PAD), rows), :] = drecv[dev * rows + hf * part + t].astype(F32)
                for i in range(rows):
                    z1_ref[pl.ds(aligned(i * seq + dev * rows + hf * part, part), part), :] += tmp[pl.ds(base + i, part, stride=pitch), :]
                return carry

            for side, first, num in ((0, -2, 5), (1, 3, chips - 5)):
                arrived = drecv.at[pl.ds(0, (num * CORES - (1 - side)) * part)]
                remote(arrived, arrived, d_ss, d_rs.at[hf, side], partner).wait_recv()
                lax.fori_loop(0, num * CORES, functools.partial(finish, first), 0)

    with jax.named_scope("drain"):
        for buf, ss, rs in ((brecv, b_ss, b_rs), (erecv, e_ss, e_rs)):
            sent(buf.at[pl.ds(0, n - 1)], ss, rs.at[0])
        sent(hsend.at[pl.ds(0, (n - 1) * rows)], h_ss, h_rs.at[0])
        sent(dsend.at[pl.ds(0, n - 1)], d_ss, d_rs.at[0, 0])


def solution(mesh):
    row_spec = P(('dp', AXIS), None, None)
    n = mesh.shape[AXIS]

    def local_fn(z, *weights):
        rows, seq, chan = z.shape
        heads = weights[1].shape[0]
        hrows = heads * rows
        part = rows // HALVES
        nq = 2 * CORES * rows
        dma = pltpu.SemaphoreType.DMA
        vmem = pl.BlockSpec(memory_space=pltpu.VMEM)
        y = pl.pallas_call(
            functools.partial(kernel, n, rows, seq, heads),
            out_shape=jax.ShapeDtypeStruct((rows * seq, chan), F32),
            in_specs=[pl.BlockSpec(memory_space=pltpu.HBM)] * 9,
            out_specs=vmem,
            scratch_shapes=[pltpu.VMEM(z.shape, z.dtype)] + [pltpu.VMEM(w.shape, w.dtype) for w in weights] + [
                pltpu.VMEM((rows, seq, chan), BF16),
                pltpu.VMEM((rows, seq, chan), BF16),
                pltpu.VMEM((rows, chan, seq), BF16),
                pltpu.VMEM((rows, seq, chan), BF16),
                pltpu.VMEM((rows, seq, chan), F32),
                pltpu.VMEM((hrows, seq), F32),
                pltpu.VMEM((n, hrows, seq), BF16),
                pltpu.VMEM((heads * nq, seq), F32),
                pltpu.VMEM((rows * (nq + PAD), chan), F32),
                pltpu.VMEM((seq, rows, chan), BF16),
                pltpu.VMEM((rows, seq, chan), BF16),
                pltpu.VMEM((n, hrows, seq), BF16),
                pltpu.VMEM((heads * seq, seq), F32),
                pltpu.VMEM((rows, seq, chan), BF16),
                pltpu.VMEM((seq, rows, chan), BF16),
                pltpu.VMEM((n * part * (rows + PAD), chan), F32),
                dma((rows // LN_UNROLL,)), dma((len(weights),)),
                dma, dma((n,)), dma, dma((n,)), dma, dma((HALVES,)), dma, dma((HALVES, 2)),
            ],
            compiler_params=pltpu.CompilerParams(collective_id=0, has_side_effects=True, vmem_limit_bytes=40 * 2 ** 20),
        )(*[pltpu.with_memory_space_constraint(a, pltpu.HBM) for a in (z,) + weights])
        return y.reshape(rows, seq, chan)

    return jax.shard_map(local_fn, mesh=mesh, in_specs=(row_spec,) + (P(),) * 8, out_specs=row_spec, check_vma=False)
```

time: 82.9 us -> 75.3 us (0.908)
  Pallas kernels: 81.2 us -> 73.9 us
  other arithmetic: 1.61 us -> 0 us
  local copies, waits for them, and re-layouts: 0 us -> 1.32 us
    pallas_call x1, Pallas kernels: 81.2 us -> 73.9 us  [local_fn(): pl.pallas_call(functools.partial(kernel, n, rows, seq, heads), out_shape=...]
    add x1 -> x0, other arithmetic: 1.61 us -> none  [local_fn(): z1.reshape(rows, seq, chan) + delta.reshape(rows, seq, chan).astype(F32)]
    unnamed x0 -> x1, local copies, waits for them, and re-layouts: none -> 1.32 us
where the time goes in v3:
time: 75.3 us; the launch traced here: 75.2 us
  Pallas kernels  73.9 us (98%)
  local copies, waits for them, and re-layouts  1.32 us (2%)
    pallas_call x1, Pallas kernels, local_fn(): pl.pallas_call(functools.partial(kernel, n, rows, seq, heads), out_shape=...  73.9 us

profile of v3, /device:TPU:21, one launch (start us, length us, event | category | flops | bytes accessed | tf_op | source)
XLA Modules:
  0.0 75.2 jit_solution(5110674009392123774)
XLA Ops:
  0.0 73.9 %shard_map.91 = f32[4096,128]{1,0:T(8,128)S(1)} custom-call(f32[16,256,128]{2,1,0:T(8,128)} %z_hbm.1, bf16[128,512]{1,0:T(8,128)(2,1)} %wps_h.1, bf16[4,128]{1,0:T(4,128)(2,1)} %wbs_h.1, bf16[128,128]{1,0:T(8,128)(2,1)} %wos_h.1, bf16[128,512]{1,0:T(8,128)(2,1)} %wpe_h.1, bf16[4,128]{1,0:T(4,128)(2,1)} %wbe_h.1, bf16[128,128]{1,0:T(8,128)(2,1)} %woe_h.1, ...), custom_call_target="tpu_custom_call" | custom-call | tf_op jit(solution)/shard_map/pallas_call | solution.py:351
  73.9 1.3 %copy.11 = f32[16,256,128]{2,1,0:T(8,128)} copy(f32[16,256,128]{2,1,0:T(8,128)S(1)} %bitcast.1) | data formatting | bytes 4194304

commit v4 on v3

--- a/solution.py
+++ b/solution.py
@@ -13,11 +13,13 @@
 AXIS = "sp"
 CORES = 2
 HALVES = 2
-COL_GROUP = 4
+COL_GROUP = 2
 HOLD_FROM = 2
 ROW_UNROLL = 8
 COL_UNROLL = 2
-LN_UNROLL = 4
+LN_UNROLL = 8
+PROJ_UNROLL = 8
+Z_ROWS = 4
 PAD = 8
 
 
@@ -64,14 +66,17 @@
         pl.semaphore_signal(barrier, 1, device_id={AXIS: lax.rem(me + off, n)}, device_id_type=MESH)
 
     def z_load(i):
-        sl = pl.ds(i * LN_UNROLL, LN_UNROLL)
+        sl = pl.ds(i * Z_ROWS, Z_ROWS)
         return pltpu.make_async_copy(z_hbm.at[sl], z_ref.at[sl], z_sem.at[i])
+
+    def z_row(r):
+        return pltpu.make_async_copy(z_hbm.at[r], z_ref.at[r], z_sem.at[r // Z_ROWS])
 
     w_loads = [pltpu.make_async_copy(src, dst, w_sem.at[i]) for i, (src, dst) in enumerate(
         [(wbs_h, wb_s), (wps_h, wp_s), (wos_h, wo_s), (wbe_h, wb_e), (wpe_h, wp_e), (woe_h, wo_e), (w1_h, w1), (w2_h, w2)])]
     w_loads[0].start()
-    for i in range(rows // LN_UNROLL):
-        z_load(i).start()
+    for r in range(rows):
+        z_row(r).start()
     for cp in w_loads[1:]:
         cp.start()
 
@@ -86,8 +91,10 @@
         def step(i, carry):
             ready(i)
             rs = [LN_UNROLL * i + t for t in range(LN_UNROLL)]
-            us = [norm(get_row(r)) for r in rs]
-            total = sum(mm(jnp.where(row_of == r, wide, 0.0).astype(BF16), u, 1, 1) for r, u in zip(rs, us))
+            us, total = [], 0.0
+            for r in rs:
+                us.append(norm(get_row(r)))
+                total += mm(jnp.where(row_of == r, wide, 0.0).astype(BF16), us[-1], 1, 1)
             if put_row is not None:
                 for r, u in zip(rs, us):
                     put_row(r, u)
@@ -100,16 +107,17 @@
     def bias_copy(buf, ss, rs, dev):
         return remote(buf.at[me], buf.at[me], ss, rs.at[me], dev)
 
-    def by_distance(dist):
-        return lax.rem(chip + ((dist + 1) // 2 if dist % 2 else chips - dist // 2), chips)
-
     def at(off):
         return lax.rem(chip + off + chips, chips)
 
-    def bias_send(buf, ss, rs):
+    def bias_send(buf, ss, rs, both):
         bias_copy(buf, ss, rs, partner).start()
-        for dist in range(1, chips):
-            bias_copy(buf, ss, rs, by_distance(dist) * CORES + core).start()
+        for off in (1, -1):
+            bias_copy(buf, ss, rs, at(off) * CORES + core).start()
+        for off in (1, -1) if both else ():
+            bias_copy(buf, ss, rs, at(off) * CORES + other).start()
+        for off in (2, -2):
+            bias_copy(buf, ss, rs, at(off) * CORES + core).start()
 
     def bias_wait(buf, ss, rs, src):
         remote(buf.at[src], buf.at[src], ss, rs.at[src], partner).wait_recv()
@@ -122,6 +130,18 @@
         bias_wait(buf, ss, rs, c * CORES + core)
         forward(buf, ss, rs, c).start()
 
+    def relay(buf, ss, rs):
+        for sign in (1, -1):
+            origin = at(-2 * sign) * CORES + core
+            bias_wait(buf, ss, rs, origin)
+            row = buf.at[origin]
+            remote(row, row, ss, rs.at[origin], at(sign) * CORES + core).start()
+
+            @pl.when(core == (1 - sign) // 2)
+            def _():
+                remote(row, row, ss, rs.at[origin], at(2 * sign) * CORES + core).start()
+            forward(buf, ss, rs, at(-2 * sign)).start()
+
     def sent(buf, ss, rs):
         remote(buf, buf, ss, rs, partner).wait_send()
 
@@ -130,19 +150,22 @@
 
     w_loads[0].wait()
     with jax.named_scope("bias_rows"):
-        pair_bias(lambda i: z_load(i).wait(), lambda r: z_ref[r], put_u, wb_s, brecv)
+        def ready(i):
+            for t in range(LN_UNROLL // Z_ROWS):
+                z_load(i * (LN_UNROLL // Z_ROWS) + t).wait()
+
+        pair_bias(ready, lambda r: z_ref[r], put_u, wb_s, brecv)
     with jax.named_scope("barrier"):
         pl.semaphore_wait(barrier, n - 1)
-    bias_send(brecv, b_ss, b_rs)
+    bias_send(brecv, b_ss, b_rs, True)
     for cp in w_loads[1:]:
         cp.wait()
 
 
     def project(i, carry):
-        for t in range(2):
-            r = 2 * i + t
-            u = u_s[r]
-            pr = mm(u, wp_s[...])
+        rs = [PROJ_UNROLL * i + t for t in range(PROJ_UNROLL)]
+        prs = [mm(u_s[r], wp_s[...]) for r in rs]
+        for r, pr in zip(rs, prs):
             q_s[r] = pr[:, :chan].astype(BF16)
             kt_s[r] = pr[:, chan:2 * chan].T.astype(BF16)
             v_s[r] = pr[:, 2 * chan:3 * chan].astype(BF16)
@@ -150,7 +173,7 @@
         return carry
 
     with jax.named_scope("project"):
-        lax.fori_loop(0, rows // 2, project, 0)
+        lax.fori_loop(0, rows // PROJ_UNROLL, project, 0)
 
     def attention(qs, kts, vs, biases, gates, wo):
         nrow = qs[0].shape[0]
@@ -210,13 +233,10 @@
 
     def fetch_ring(dist):
         fetch(brecv, b_ss, b_rs, at(dist))
-        if isinstance(dist, int):
-            if 2 * dist % chips:
-                fetch(brecv, b_ss, b_rs, at(-dist))
-        else:
-            @pl.when(2 * dist < chips)
-            def _():
-                fetch(brecv, b_ss, b_rs, at(-dist))
+
+        @pl.when(2 * dist < chips)
+        def _():
+            fetch(brecv, b_ss, b_rs, at(-dist))
 
     def send_ring(cs, hf):
         for s in range(CORES):
@@ -224,7 +244,9 @@
                 h_copy(c * CORES + s, hf).start()
 
     bias_wait(brecv, b_ss, b_rs, partner)
-    start_block([chip], lambda: fetch_ring(1))
+    start_block([chip], lambda: None)
+    for off in (1, -1):
+        bias_wait(brecv, b_ss, b_rs, at(off) * CORES + core)
     for hf in range(HALVES):
         h_copy(partner, hf).start()
 
@@ -232,7 +254,16 @@
         cs = [at(dist), at(-dist)]
         for c in cs:
             wait_other(c)
-        start_block(cs, lambda: fetch_ring(dist + 1))
+        def between():
+            @pl.when(dist == 1)
+            def _():
+                relay(brecv, b_ss, b_rs)
+
+            @pl.when(dist > 1)
+            def _():
+                fetch_ring(dist + 1)
+
+        start_block(cs, between)
         send_ring(cs, 0)
         for hf in range(1, HALVES):
             @pl.when(dist < HOLD_FROM)
@@ -244,20 +275,21 @@
     lax.fori_loop(1, far, start_ring, 0)
     wait_other(at(far))
     start_block([at(far)], lambda: None)
-    send_ring([at(far)], 0)
 
     with jax.named_scope("bias_cols"):
         pair_bias(lambda i: None, lambda r: z1_ref[pl.ds(aligned(r * seq, seq), seq), :].astype(BF16).astype(F32), None, wb_e, erecv)
-    bias_send(erecv, e_ss, e_rs)
-    for hf in range(1, HALVES):
-        for dist in range(HOLD_FROM, far):
-            send_ring([at(dist), at(-dist)], hf)
-        send_ring([at(far)], hf)
+    bias_send(erecv, e_ss, e_rs, False)
+    send_ring([at(far)], 0)
     ht[:, pl.ds(aligned(me * rows, rows), rows), :] = hsend[pl.ds(aligned(me * rows, rows), rows)]
 
     with jax.named_scope("wait_cols"):
-        for dist in range(1, chips):
-            fetch(erecv, e_ss, e_rs, by_distance(dist))
+        relay(erecv, e_ss, e_rs)
+        for hf in range(1, HALVES):
+            for dist in range(HOLD_FROM, far):
+                send_ring([at(dist), at(-dist)], hf)
+            send_ring([at(far)], hf)
+        for off in (1, -1, 3, -3, 4):
+            fetch(erecv, e_ss, e_rs, at(off))
         for c in range(chips):
             bias_wait(erecv, e_ss, e_rs, c * CORES + other)
 
@@ -370,7 +402,7 @@
                 pltpu.VMEM((rows, seq, chan), BF16),
                 pltpu.VMEM((seq, rows, chan), BF16),
                 pltpu.VMEM((n * part * (rows + PAD), chan), F32),
-                dma((rows // LN_UNROLL,)), dma((len(weights),)),
+                dma((rows // Z_ROWS,)), dma((len(weights),)),
                 dma, dma((n,)), dma, dma((n,)), dma, dma((HALVES,)), dma, dma((HALVES, 2)),
             ],
             compiler_params=pltpu.CompilerParams(collective_id=0, has_side_effects=True, vmem_limit_bytes=40 * 2 ** 20),

time: 75.3 us -> 72.1 us (0.958)
  Pallas kernels: 73.9 us -> 70.7 us
    pallas_call x1, Pallas kernels: 73.9 us -> 70.7 us  [local_fn(): pl.pallas_call(functools.partial(kernel, n, rows, seq, heads), out_shape=...]
where the time goes in v4:
time: 72.1 us; the launch traced here: 72 us
  Pallas kernels  70.7 us (98%)
  local copies, waits for them, and re-layouts  1.32 us (2%)
    pallas_call x1, Pallas kernels, local_fn(): pl.pallas_call(functools.partial(kernel, n, rows, seq, heads), out_shape=...  70.7 us

profile of v4, /device:TPU:21, one launch (start us, length us, event | category | flops | bytes accessed | tf_op | source)
XLA Modules:
  0.0 72.0 jit_solution(2130292507715664558)
XLA Ops:
  0.0 70.7 %shard_map.91 = f32[4096,128]{1,0:T(8,128)S(1)} custom-call(f32[16,256,128]{2,1,0:T(8,128)} %z_hbm.1, bf16[128,512]{1,0:T(8,128)(2,1)} %wps_h.1, bf16[4,128]{1,0:T(4,128)(2,1)} %wbs_h.1, bf16[128,128]{1,0:T(8,128)(2,1)} %wos_h.1, bf16[128,512]{1,0:T(8,128)(2,1)} %wpe_h.1, bf16[4,128]{1,0:T(4,128)(2,1)} %wbe_h.1, bf16[128,128]{1,0:T(8,128)(2,1)} %woe_h.1, ...), custom_call_target="tpu_custom_call" | custom-call | tf_op jit(solution)/shard_map/pallas_call | solution.py:383
  70.7 1.3 %copy.11 = f32[16,256,128]{2,1,0:T(8,128)} copy(f32[16,256,128]{2,1,0:T(8,128)S(1)} %bitcast.1) | data formatting | bytes 4194304

commit v5 on v4

--- a/solution.py
+++ b/solution.py
@@ -62,8 +62,9 @@
         return pl.multiple_of(i, k)
 
     barrier = pltpu.get_barrier_semaphore()
-    for off in range(1, n):
-        pl.semaphore_signal(barrier, 1, device_id={AXIS: lax.rem(me + off, n)}, device_id_type=MESH)
+    greeted = [partner] + [lax.rem(chip + off + chips, chips) * CORES + s for off in (1, -1, 2, -2) for s in range(CORES)]
+    for dev in greeted:
+        pl.semaphore_signal(barrier, 1, device_id={AXIS: dev}, device_id_type=MESH)
 
     def z_load(i):
         sl = pl.ds(i * Z_ROWS, Z_ROWS)
@@ -156,7 +157,7 @@
 
         pair_bias(ready, lambda r: z_ref[r], put_u, wb_s, brecv)
     with jax.named_scope("barrier"):
-        pl.semaphore_wait(barrier, n - 1)
+        pl.semaphore_wait(barrier, len(greeted))
     bias_send(brecv, b_ss, b_rs, True)
     for cp in w_loads[1:]:
         cp.wait()

time: 72.1 us -> 73.2 us (1.015)
  the two profiles are of different devices: /device:TPU:21 before, /device:TPU:29 now
where the time goes in v5:
time: 73.2 us; the launch traced here: 73.1 us
  Pallas kernels  71.8 us (98%)
  local copies, waits for them, and re-layouts  1.32 us (2%)
    pallas_call x1, Pallas kernels, local_fn(): pl.pallas_call(functools.partial(kernel, n, rows, seq, heads), out_shape=...  71.8 us

profile of v5, /device:TPU:29, one launch (start us, length us, event | category | flops | bytes accessed | tf_op | source)
XLA Modules:
  0.0 73.1 jit_solution(10563432136504426985)
XLA Ops:
  0.0 71.8 %shard_map.91 = f32[4096,128]{1,0:T(8,128)S(1)} custom-call(f32[16,256,128]{2,1,0:T(8,128)} %z_hbm.1, bf16[128,512]{1,0:T(8,128)(2,1)} %wps_h.1, bf16[4,128]{1,0:T(4,128)(2,1)} %wbs_h.1, bf16[128,128]{1,0:T(8,128)(2,1)} %wos_h.1, bf16[128,512]{1,0:T(8,128)(2,1)} %wpe_h.1, bf16[4,128]{1,0:T(4,128)(2,1)} %wbe_h.1, bf16[128,128]{1,0:T(8,128)(2,1)} %woe_h.1, ...), custom_call_target="tpu_custom_call" | custom-call | tf_op jit(solution)/shard_map/pallas_call | solution.py:384
  71.8 1.3 %copy.11 = f32[16,256,128]{2,1,0:T(8,128)} copy(f32[16,256,128]{2,1,0:T(8,128)S(1)} %bitcast.1) | data formatting | bytes 4194304

commit v6 on v5

--- a/solution.py
+++ b/solution.py
@@ -17,9 +17,8 @@
 HOLD_FROM = 2
 ROW_UNROLL = 8
 COL_UNROLL = 2
-LN_UNROLL = 8
+LN_ROWS = 4
 PROJ_UNROLL = 8
-Z_ROWS = 4
 PAD = 8
 
 
@@ -41,8 +40,9 @@
 def kernel(n, rows, seq, heads, z_hbm, wps_h, wbs_h, wos_h, wpe_h, wbe_h, woe_h, w1_h, w2_h,
            z1_ref,
            z_ref, wp_s, wb_s, wo_s, wp_e, wb_e, wo_e, w1, w2,
-           u_s, q_s, kt_s, v_s, g_s, bacc, brecv, bias_f, zb, hsend, ht, erecv, bias_e, dsend, drecv, tmp,
+           u_s, q_s, kt_s, v_s, g_s, cen_a, cen_b, brecv, bias_f, zb, hsend, ht, erecv, bias_e, dsend, drecv, tmp,
            z_sem, w_sem, b_ss, b_rs, e_ss, e_rs, h_ss, h_rs, d_ss, d_rs):
+    cen = (cen_a, cen_b)
     chan = wo_s.shape[0]
     hd = chan // heads
     scale = hd ** -0.5
@@ -61,17 +61,12 @@
     def aligned(i, k):
         return pl.multiple_of(i, k)
 
-    barrier = pltpu.get_barrier_semaphore()
-    greeted = [partner] + [lax.rem(chip + off + chips, chips) * CORES + s for off in (1, -1, 2, -2) for s in range(CORES)]
-    for dev in greeted:
-        pl.semaphore_signal(barrier, 1, device_id={AXIS: dev}, device_id_type=MESH)
-
     def z_load(i):
-        sl = pl.ds(i * Z_ROWS, Z_ROWS)
+        sl = pl.ds(i * LN_ROWS, LN_ROWS)
         return pltpu.make_async_copy(z_hbm.at[sl], z_ref.at[sl], z_sem.at[i])
 
     def z_row(r):
-        return pltpu.make_async_copy(z_hbm.at[r], z_ref.at[r], z_sem.at[r // Z_ROWS])
+        return pltpu.make_async_copy(z_hbm.at[r], z_ref.at[r], z_sem.at[r // LN_ROWS])
 
     w_loads = [pltpu.make_async_copy(src, dst, w_sem.at[i]) for i, (src, dst) in enumerate(
         [(wbs_h, wb_s), (wps_h, wp_s), (wos_h, wo_s), (wbe_h, wb_e), (wpe_h, wp_e), (woe_h, wo_e), (w1_h, w1), (w2_h, w2)])]
@@ -81,29 +76,35 @@
     for cp in w_loads[1:]:
         cp.start()
 
+    barrier = pltpu.get_barrier_semaphore()
+    greeted = [partner] + [lax.rem(chip + off + chips, chips) * CORES + s for off in (1, -1, 2, -2) for s in range(CORES)]
+    for dev in greeted:
+        pl.semaphore_signal(barrier, 1, device_id={AXIS: dev}, device_id_type=MESH)
+
     row_of = lax.rem(lax.broadcasted_iota(jnp.int32, (hrows, chan), 0), rows)
     lane_head = lax.broadcasted_iota(jnp.int32, (1, chan), 1) // hd
 
     def pair_bias(ready, get_row, put_row, wb, out):
         wide = wb[...].astype(F32)
         wide = jnp.concatenate([jnp.broadcast_to(wide[h:h + 1], (rows, chan)) for h in range(heads)], axis=0)
-        bacc[...] = jnp.zeros_like(bacc)
-
-        def step(i, carry):
-            ready(i)
-            rs = [LN_UNROLL * i + t for t in range(LN_UNROLL)]
-            us, total = [], 0.0
-            for r in rs:
-                us.append(norm(get_row(r)))
-                total += mm(jnp.where(row_of == r, wide, 0.0).astype(BF16), us[-1], 1, 1)
-            if put_row is not None:
-                for r, u in zip(rs, us):
-                    put_row(r, u)
-            bacc[...] += total
-            return carry
-
-        lax.fori_loop(0, rows // LN_UNROLL, step, 0)
-        out[me] = bacc[...].astype(BF16)
+        total = jnp.zeros((hrows, seq), F32)
+        steps = rows // LN_ROWS
+        for i in range(steps + 1):
+            if i < steps:
+                ready(i)
+                for t in range(LN_ROWS):
+                    vals = get_row(i * LN_ROWS + t)
+                    cen[i % 2][t] = vals - jnp.mean(vals, axis=-1, keepdims=True)
+            if i:
+                for t in range(LN_ROWS):
+                    r = (i - 1) * LN_ROWS + t
+                    centered = cen[(i - 1) % 2][t]
+                    variance = jnp.mean(centered * centered, axis=-1, keepdims=True)
+                    u = (centered * lax.rsqrt(variance + LN_EPS)).astype(BF16)
+                    if put_row is not None:
+                        put_row(r, u)
+                    total += mm(jnp.where(row_of == r, wide, 0.0).astype(BF16), u, 1, 1)
+        out[me] = total.astype(BF16)
 
     def bias_copy(buf, ss, rs, dev):
         return remote(buf.at[me], buf.at[me], ss, rs.at[me], dev)
@@ -151,11 +152,7 @@
 
     w_loads[0].wait()
     with jax.named_scope("bias_rows"):
-        def ready(i):
-            for t in range(LN_UNROLL // Z_ROWS):
-                z_load(i * (LN_UNROLL // Z_ROWS) + t).wait()
-
-        pair_bias(ready, lambda r: z_ref[r], put_u, wb_s, brecv)
+        pair_bias(lambda i: z_load(i).wait(), lambda r: z_ref[r], put_u, wb_s, brecv)
     with jax.named_scope("barrier"):
         pl.semaphore_wait(barrier, len(greeted))
     bias_send(brecv, b_ss, b_rs, True)
@@ -392,7 +389,7 @@
                 pltpu.VMEM((rows, chan, seq), BF16),
                 pltpu.VMEM((rows, seq, chan), BF16),
                 pltpu.VMEM((rows, seq, chan), F32),
-                pltpu.VMEM((hrows, seq), F32),
+                pltpu.VMEM((LN_ROWS, seq, chan), F32), pltpu.VMEM((LN_ROWS, seq, chan), F32),
                 pltpu.VMEM((n, hrows, seq), BF16),
                 pltpu.VMEM((heads * nq, seq), F32),
                 pltpu.VMEM((rows * (nq + PAD), chan), F32),
@@ -403,7 +400,7 @@
                 pltpu.VMEM((rows, seq, chan), BF16),
                 pltpu.VMEM((seq, rows, chan), BF16),
                 pltpu.VMEM((n * part * (rows + PAD), chan), F32),
-                dma((rows // Z_ROWS,)), dma((len(weights),)),
+                dma((rows // LN_ROWS,)), dma((len(weights),)),
                 dma, dma((n,)), dma, dma((n,)), dma, dma((HALVES,)), dma, dma((HALVES, 2)),
             ],
             compiler_params=pltpu.CompilerParams(collective_id=0, has_side_effects=True, vmem_limit_bytes=40 * 2 ** 20),

time: 73.2 us -> 70.7 us (0.966)
  the two profiles are of different devices: /device:TPU:29 before, /device:TPU:21 now
where the time goes in v6:
time: 70.7 us; the launch traced here: 70.6 us
  Pallas kernels  69.3 us (98%)
  local copies, waits for them, and re-layouts  1.32 us (2%)
    pallas_call x1, Pallas kernels, local_fn(): pl.pallas_call(functools.partial(kernel, n, rows, seq, heads), out_shape=...  69.3 us

profile of v6, /device:TPU:21, one launch (start us, length us, event | category | flops | bytes accessed | tf_op | source)
XLA Modules:
  0.0 70.6 jit_solution(16448680372257858336)
XLA Ops:
  0.0 69.3 %shard_map.91 = f32[4096,128]{1,0:T(8,128)S(1)} custom-call(f32[16,256,128]{2,1,0:T(8,128)} %z_hbm.1, bf16[128,512]{1,0:T(8,128)(2,1)} %wps_h.1, bf16[4,128]{1,0:T(4,128)(2,1)} %wbs_h.1, bf16[128,128]{1,0:T(8,128)(2,1)} %wos_h.1, bf16[128,512]{1,0:T(8,128)(2,1)} %wpe_h.1, bf16[4,128]{1,0:T(4,128)(2,1)} %wbe_h.1, bf16[128,128]{1,0:T(8,128)(2,1)} %woe_h.1, ...), custom_call_target="tpu_custom_call" | custom-call | tf_op jit(solution)/shard_map/pallas_call | solution.py:381
  69.3 1.3 %copy.11 = f32[16,256,128]{2,1,0:T(8,128)} copy(f32[16,256,128]{2,1,0:T(8,128)S(1)} %bitcast.1) | data formatting | bytes 4194304

commit v7 on v6

--- a/solution.py
+++ b/solution.py
@@ -299,14 +299,13 @@
     with jax.named_scope("widen"):
         lax.fori_loop(0, heads, widen, 0)
 
-    def is_far(off):
-        return int(min(off // CORES, chips - off // CORES) > 2)
-
-    def d_copy(off, grp):
+    def ring_dist(off):
+        return min(off // CORES, chips - off // CORES)
+
+    def d_copy(off, first, count, hf):
         dev = lax.rem(me // CORES * CORES + off // CORES * CORES, n) + (core if off % CORES == 0 else other)
-        return remote(dsend.at[pl.ds(grp * COL_GROUP, COL_GROUP), pl.ds(aligned(dev * rows, rows), rows), :],
-                      drecv.at[pl.ds(me * rows + grp * COL_GROUP, COL_GROUP)],
-                      d_ss, d_rs.at[grp // (part // COL_GROUP), is_far(off)], dev)
+        return remote(dsend.at[pl.ds(first, count), pl.ds(aligned(dev * rows, rows), rows), :],
+                      drecv.at[pl.ds(me * rows + first, count)], d_ss, d_rs.at[hf, int(ring_dist(off) > 2)], dev)
 
     def end_cols(i, carry):
         js = [COL_UNROLL * i + t for t in range(COL_UNROLL)]
@@ -323,7 +322,7 @@
             dsend[j] = (e + t).astype(BF16)
         return carry
 
-    far_first = sorted(range(1, n), key=lambda off: -min(off // CORES, chips - off // CORES))
+    far_first = sorted(range(1, n), key=lambda off: -ring_dist(off))
     per = COL_GROUP // COL_UNROLL
 
     def end_group(grp, carry):
@@ -336,10 +335,15 @@
         with jax.named_scope("end_cols"):
             lax.fori_loop(grp * per, (grp + 1) * per, end_cols, 0)
         for off in far_first:
-            d_copy(off, grp).start()
+            if ring_dist(off) != 1:
+                d_copy(off, grp * COL_GROUP, COL_GROUP, grp // (part // COL_GROUP)).start()
         return carry
 
     lax.fori_loop(0, rows // COL_GROUP, end_group, 0)
+    for hf in range(HALVES):
+        for off in far_first:
+            if ring_dist(off) == 1:
+                d_copy(off, hf * part, part, hf).start()
     drecv[pl.ds(me * rows, rows)] = dsend[:, pl.ds(aligned(me * rows, rows), rows), :]
 
     pitch = rows + PAD

time: 70.7 us -> 70.3 us (level)
  no operation moved by 1% of the time
where the time goes in v7:
time: 70.3 us; the launch traced here: 70.2 us
  Pallas kernels  68.9 us (98%)
  local copies, waits for them, and re-layouts  1.32 us (2%)
    pallas_call x1, Pallas kernels, local_fn(): pl.pallas_call(functools.partial(kernel, n, rows, seq, heads), out_shape=...  68.9 us

profile of v7, /device:TPU:21, one launch (start us, length us, event | category | flops | bytes accessed | tf_op | source)
XLA Modules:
  0.0 70.2 jit_solution(11487392097573941004)
XLA Ops:
  0.0 68.9 %shard_map.91 = f32[4096,128]{1,0:T(8,128)S(1)} custom-call(f32[16,256,128]{2,1,0:T(8,128)} %z_hbm.1, bf16[128,512]{1,0:T(8,128)(2,1)} %wps_h.1, bf16[4,128]{1,0:T(4,128)(2,1)} %wbs_h.1, bf16[128,128]{1,0:T(8,128)(2,1)} %wos_h.1, bf16[128,512]{1,0:T(8,128)(2,1)} %wpe_h.1, bf16[4,128]{1,0:T(4,128)(2,1)} %wbe_h.1, bf16[128,128]{1,0:T(8,128)(2,1)} %woe_h.1, ...), custom_call_target="tpu_custom_call" | custom-call | tf_op jit(solution)/shard_map/pallas_call | solution.py:385
  68.9 1.3 %copy.11 = f32[16,256,128]{2,1,0:T(8,128)} copy(f32[16,256,128]{2,1,0:T(8,128)S(1)} %bitcast.1) | data formatting | bytes 4194304
